TPU v7x, 32 devices: a whole 2x2x4 slice. The times are simulated.
32 devices in a mesh: gx: 8 (over y, x, core), gy: 4 (over z).
Axes of the slice: x: 2, y: 2, z: 4, core: 2. Of those that a mesh axis runs over, the one named last changes fastest.
Arguments:
- right_side: float32 [128, 256, 192], P('gx', 'gy'), may hold values from -46 to 46
- diagonal: float32 [128, 256, 192], P('gx', 'gy'), may hold values from 0.1 to 2
Outputs:
- solution_field: float32 [128, 256, 192], P('gx', 'gy')
- residual: float32 [128, 256, 192], P('gx', 'gy')
All inputs are finite; a program needn't handle non-finite values.
Results may differ from a plain program's by a relative error of at most 0.00017.
Values sent between devices are 32-bit elements; how exact they have to be, the bound alone decides.
A program may use at most 64 MiB of HBM per device.

v0:
```python
import functools

import jax
import jax.numpy as jnp
from jax import lax
from jax.experimental import pallas as pl
from jax.experimental.pallas import tpu as pltpu
from jax.sharding import PartitionSpec as P

ITERS = 3
SHIFT = 7.0
MESH = pl.DeviceIdType.MESH
DIRS = ((1, 0), (-1, 0), (0, 1), (0, -1), (1, 1), (1, -1), (-1, 1), (-1, -1))
RIM = ITERS
ROWS = 8


def span_x(step, width, size):
    if step == 0:
        return pl.ds(0, size), pl.ds(RIM, size)
    if step > 0:
        return pl.ds(size - width, width), pl.ds(RIM - width, width)
    return pl.ds(0, width), pl.ds(RIM + size, width)


def span_y(step, width, size):
    if step == 0:
        return pl.ds(0, size), pl.ds(ROWS, size)
    if step > 0:
        return pl.ds(size - width, width), pl.ds(ROWS - width, width)
    return pl.ds(0, width), pl.ds(ROWS + size, width)


def times_b(field, shift, layer, valid, span=slice(None)):
    here = field[layer, span]
    rows, lanes = here.shape
    row0 = jnp.zeros((1, lanes), jnp.float32)
    lane0 = jnp.zeros((rows, 1), jnp.float32)
    beside = field[layer - 1, span] + field[layer + 1, span]
    beside = beside + jnp.concatenate([here[1:], row0], 0)
    beside = beside + jnp.concatenate([row0, here[:-1]], 0)
    beside = beside + jnp.concatenate([here[:, 1:], lane0], 1)
    beside = beside + jnp.concatenate([lane0, here[:, :-1]], 1)
    out = (shift[layer, span] + (6.0 - SHIFT)) * here - beside
    if valid is None:
        return out
    return jnp.where(valid, out, 0.0)


def coefficients(moments):
    def inner(f, g):
        total = None
        for i, a in enumerate(f):
            for j, c in enumerate(g):
                term = a * c * moments[i + j]
                total = term if total is None else total + term
        return total

    def times_a(f):
        out = [SHIFT * f[0]]
        for k in range(1, len(f)):
            out.append(SHIFT * f[k] + f[k - 1])
        return out + [f[-1]]

    def axpy(f, a, g):
        size = max(len(f), len(g))
        out = []
        for k in range(size):
            if k >= len(f):
                out.append(a * g[k])
            elif k >= len(g):
                out.append(f[k])
            else:
                out.append(f[k] + a * g[k])
        return out

    one = jnp.ones_like(moments[0])
    residual, solution_field = [one], []
    s_field, p_field = [], []
    for step in range(ITERS):
        w_field = times_a(residual)
        gamma = inner(residual, residual)
        delta = inner(w_field, residual)
        if step == 0:
            alpha = gamma / delta
            s_field, p_field = w_field, residual
        else:
            beta = gamma / gamma_prev
            alpha = gamma / (delta - beta * gamma / alpha_prev)
            s_field = axpy(w_field, beta, s_field)
            p_field = axpy(residual, beta, p_field)
        solution_field = axpy(solution_field, alpha, p_field)
        residual = axpy(residual, -alpha, s_field)
        gamma_prev, alpha_prev = gamma, alpha
    return solution_field + residual


def kernel(nx, ny, b_ref, d_ref, v1_ref, v2_ref, v3_ref, co_ref,
           v0, dd, v1, v2, part, slots,
           tail_out, tail_in, own_sem, send_sem, recv_sem, sum_send, sum_recv, tail_send, tail_recv):
    gx, gy = lax.axis_index("gx"), lax.axis_index("gy")
    bx, by, bz = b_ref.shape
    barrier = pltpu.get_barrier_semaphore()

    def there(dx, dy):
        ok = None
        for at, step, count in ((gx, dx, nx), (gy, dy, ny)):
            if step:
                this = (at + step >= 0) & (at + step < count)
                ok = this if ok is None else ok & this
        return ok

    def peer_x(k):
        return lax.rem(gx + k, nx)

    def peer_y(k):
        return lax.rem(gy + k, ny)

    count = nx * ny
    me = gx * ny + gy

    def peer(k):
        to = lax.rem(me + k, count)
        return to // ny, lax.rem(to, ny)

    @pl.loop(1, count)
    def _(k):
        pl.semaphore_signal(barrier, inc=1, device_id=peer(k), device_id_type=MESH)

    own = []
    for n, (src, dst) in enumerate(((b_ref, v0), (d_ref, dd))):
        own.append(pltpu.make_async_copy(
            src, dst.at[pl.ds(RIM, bx), pl.ds(ROWS, by), :], own_sem.at[n]))
        own[-1].start()

    @pl.when(gx == 0)
    def _():
        v0[0:RIM] = jnp.zeros((RIM,) + v0.shape[1:], jnp.float32)

    @pl.when(gx == nx - 1)
    def _():
        v0[RIM + bx:] = jnp.zeros((RIM,) + v0.shape[1:], jnp.float32)

    @pl.when(gy == 0)
    def _():
        v0[:, 0:ROWS] = jnp.zeros((v0.shape[0], ROWS, bz), jnp.float32)

    @pl.when(gy == ny - 1)
    def _():
        v0[:, ROWS + by:] = jnp.zeros((v0.shape[0], ROWS, bz), jnp.float32)

    def halo(n, dx, dy):
        width = RIM - n if dx == 0 or dy == 0 else RIM - 1 - n
        width_y = width
        dst = (v0, dd)[n]
        src = dst.at[pl.ds(RIM, bx), pl.ds(ROWS, by), :]
        from_x, to_x = span_x(dx, width, bx)
        from_y, to_y = span_y(dy, width_y, by)
        index = DIRS.index((dx, dy))
        lanes = pl.ds(0, bz // 128 * 128) if dy == 0 else slice(None)
        return pltpu.make_async_remote_copy(
            src_ref=src.at[from_x, from_y, lanes],
            dst_ref=dst.at[to_x, to_y, lanes],
            send_sem=send_sem.at[n, index],
            recv_sem=recv_sem.at[n, index],
            device_id=(gx + dx, gy + dy),
            device_id_type=MESH,
        )

    for copy in own:
        copy.wait()
    full = bz // 128 * 128
    tail = bz - full
    half = by // 2
    last = pl.ds(full, tail)

    def tails(dx, sending):
        first, second = pl.ds(0, tail), pl.ds(tail, tail)
        low = {(True, 1): RIM + bx - 1, (True, -1): RIM, (False, 1): RIM - 1,
               (False, -1): RIM + bx}[sending, dx]
        at = [low - dx * k for k in range(RIM)]
        every = pl.ds(ROWS, by)
        return (
            (v0, at[0], every, pl.ds(0, by), first),
            (v0, at[1], every, pl.ds(0, by), second),
            (v0, at[2], every, pl.ds(by, by), first),
            (dd, at[0], every, pl.ds(by, by), second),
            (dd, at[1], pl.ds(ROWS, half), pl.ds(2 * by, half), first),
            (dd, at[1], pl.ds(ROWS + half, half), pl.ds(2 * by, half), second),
        )

    for side, dx in enumerate((1, -1)):
        for array, layer, rows, to, lanes in tails(dx, True):
            tail_out[side, to, lanes] = array[layer, rows, last]

    def tail_copy(dx):
        side = (1, -1).index(dx)
        return pltpu.make_async_remote_copy(
            src_ref=tail_out.at[side], dst_ref=tail_in.at[side], send_sem=tail_send.at[side],
            recv_sem=tail_recv.at[side], device_id=(gx + dx, gy), device_id_type=MESH)

    def unpack(dx):
        side = (1, -1).index(dx)
        for array, layer, rows, to, lanes in tails(dx, False):
            array[layer, rows, last] = tail_in[side, to, lanes]

    pl.semaphore_wait(barrier, count - 1)

    for n in range(2):
        for dx, dy in DIRS:
            @pl.when(there(dx, dy))
            def _(n=n, dx=dx, dy=dy):
                halo(n, dx, dy).start()

    for dx in (1, -1):
        @pl.when(there(dx, 0))
        def _(dx=dx):
            tail_copy(dx).start()

    def arrived(directions):
        for n in range(2):
            for dx, dy in directions:
                @pl.when(there(-dx, -dy))
                def _(n=n, dx=dx, dy=dy):
                    halo(n, dx, dy).wait_recv()

    row = lax.broadcasted_iota(jnp.int32, (by + 2 * ROWS, bz), 0)
    inside_y = ((row >= ROWS) | (gy > 0)) & ((row < ROWS + by) | (gy < ny - 1))

    def inside(layer):
        ok = ((layer >= RIM) | (gx > 0)) & ((layer < RIM + bx) | (gx < nx - 1))
        return inside_y & ok

    inner = slice(ROWS, ROWS + by)

    def add_up(layer, span, f3, sums):
        k = layer - RIM
        rows = slice(span.start - ROWS, span.stop - ROWS)
        f0, f1, f2 = v0[layer, span], v1[layer, span], v2[layer, span]
        v1_ref[k, rows] = f1
        v2_ref[k, rows] = f2
        v3_ref[k, rows] = f3
        pairs = (f0 * f0, f0 * f1, f1 * f1, f1 * f2, f2 * f2, f2 * f3)
        groups = (span.stop - span.start) // 8
        return tuple(s + jnp.sum(p.reshape(groups, 8, bz), 0) for s, p in zip(sums, pairs))

    def body(layer, sums):
        return add_up(layer, inner, times_b(v2, dd, layer, None)[inner], sums)

    def stencils(starts, count, valid, sums):
        @pl.loop(0, count[0], unroll=True)
        def _(k):
            layer = starts[0] + k
            v1[layer] = times_b(v0, dd, layer, valid(layer))

        @pl.loop(0, count[1], unroll=True)
        def _(k):
            layer = starts[1] + k
            v2[layer] = times_b(v1, dd, layer, valid(layer))

        return lax.fori_loop(0, count[2], lambda k, s: body(starts[2] + k, s), sums, unroll=True)

    sums = (jnp.zeros((8, bz), jnp.float32),) * 6

    @pl.loop(RIM + 1, RIM + bx - 1, unroll=2)
    def _(layer):
        v1[layer, inner] = times_b(v0, dd, layer, None, inner)

    @pl.loop(RIM + 2, RIM + bx - 2, unroll=2)
    def _(layer):
        v2[layer, inner] = times_b(v1, dd, layer, None, inner)

    middle = slice(2 * ROWS, by)

    def middle_rows(layer, sums):
        f3 = times_b(v2, dd, layer, None, inner)[ROWS:by - ROWS]
        return add_up(layer, middle, f3, sums)

    sums = lax.fori_loop(RIM + 3, RIM + bx - 3, middle_rows, sums, unroll=2)

    arrived(DIRS[2:4])
    low_rows, high_rows = slice(0, 3 * ROWS), slice(by - ROWS, by + 2 * ROWS)
    low_in, high_in = gy > 0, gy < ny - 1
    short = lax.broadcasted_iota(jnp.int32, (3 * ROWS, bz), 0)
    low_ok = (short >= ROWS) | low_in
    high_ok = (short < 2 * ROWS) | high_in

    def ends(field, out, layer):
        out[layer, 0:2 * ROWS] = times_b(field, dd, layer, low_ok, low_rows)[:2 * ROWS]
        out[layer, by:by + 2 * ROWS] = times_b(field, dd, layer, high_ok, high_rows)[ROWS:]

    @pl.loop(RIM + 1, RIM + bx - 1, unroll=2)
    def _(layer):
        ends(v0, v1, layer)

    @pl.loop(RIM + 2, RIM + bx - 2, unroll=2)
    def _(layer):
        ends(v1, v2, layer)

    def end_rows(layer, sums):
        f3 = times_b(v2, dd, layer, None, low_rows)[ROWS:2 * ROWS]
        sums = add_up(layer, slice(ROWS, 2 * ROWS), f3, sums)
        f3 = times_b(v2, dd, layer, None, high_rows)[ROWS:2 * ROWS]
        return add_up(layer, slice(by, by + ROWS), f3, sums)

    sums = lax.fori_loop(RIM + 3, RIM + bx - 3, end_rows, sums, unroll=2)
    near_high = lax.rem(gx, 2) == 0
    for turn in range(2):
        high = near_high if turn == 0 else jnp.logical_not(near_high)

        @pl.when(high)
        def _():
            arrived([d for d in DIRS if d[0] < 0])

            @pl.when(there(1, 0))
            def _():
                tail_copy(-1).wait_recv()
                unpack(-1)

        @pl.when(jnp.logical_not(high))
        def _():
            arrived([d for d in DIRS if d[0] > 0])

            @pl.when(there(-1, 0))
            def _():
                tail_copy(1).wait_recv()
                unpack(1)

        starts = tuple(jnp.where(high, RIM + bx - 1 - k, RIM - 2 + k) for k in range(3))
        sums = stencils(starts, (3, 3, 3), inside, sums)

    lane = [jnp.sum(jnp.sum(s, 1, keepdims=True), 0, keepdims=True) for s in sums]
    lane_of = lax.broadcasted_iota(jnp.int32, (1, 128), 1)
    packed = jnp.zeros((1, 128), jnp.float32)
    for k, s in enumerate(lane):
        packed = jnp.where(lane_of == k, s, packed)
    part[0] = packed

    @pl.loop(1, count)
    def _(k):
        pltpu.make_async_remote_copy(
            src_ref=part.at[0], dst_ref=slots.at[me], send_sem=sum_send.at[0],
            recv_sem=sum_recv.at[0], device_id=peer(k), device_id_type=MESH).start()

    slots[me] = packed
    others = slots.at[pl.ds(0, count - 1)]
    pltpu.make_async_copy(others, others, sum_recv.at[0]).wait()
    total = jnp.sum(slots[...], 0)
    moments = [total[:, k:k + 1] for k in range(6)]
    row8 = lax.broadcasted_iota(jnp.int32, (8, 128), 0)
    co = jnp.zeros((8, 128), jnp.float32)
    for k, c in enumerate(coefficients(moments)):
        co = jnp.where(row8 == k, c, co)
    co_ref[...] = co
    pltpu.make_async_copy(others, others, sum_send.at[0]).wait()

    for n in range(2):
        for dx, dy in DIRS:
            @pl.when(there(dx, dy))
            def _(n=n, dx=dx, dy=dy):
                halo(n, dx, dy).wait_send()

    for dx in (1, -1):
        @pl.when(there(dx, 0))
        def _(dx=dx):
            tail_copy(dx).wait_send()


def combine(f0_ref, f1_ref, f2_ref, f3_ref, co_ref, x_ref, r_ref, x_out, r_out, sems):
    c = [co_ref[k:k + 1, 0:1] for k in range(7)]
    count = x_out.shape[0]

    def copy(n, k):
        src, dst = ((x_out, x_ref), (r_out, r_ref))[n]
        return pltpu.make_async_copy(src.at[pl.ds(k, 1)], dst.at[pl.ds(k, 1)], sems.at[n, k])

    @pl.loop(0, count)
    def _(k):
        f0, f1, f2, f3 = f0_ref[k], f1_ref[k], f2_ref[k], f3_ref[k]
        x_out[k] = c[0] * f0 + c[1] * f1 + c[2] * f2
        r_out[k] = c[3] * f0 + c[4] * f1 + c[5] * f2 + c[6] * f3
        for n in range(2):
            copy(n, k).start()

    @pl.loop(0, count)
    def _(k):
        for n in range(2):
            copy(n, k).wait()


def on_device(nx, ny, right_side, diagonal):
    bx, by, bz = right_side.shape
    block = jax.ShapeDtypeStruct((bx, by, bz), jnp.float32)
    big = pltpu.VMEM((bx + 2 * RIM, by + 2 * ROWS, bz), jnp.float32)
    vmem = pl.BlockSpec(memory_space=pltpu.VMEM)
    dma = pltpu.SemaphoreType.DMA
    f1, f2, f3, co = pl.pallas_call(
        functools.partial(kernel, nx, ny),
        out_shape=(block, block, block, jax.ShapeDtypeStruct((8, 128), jnp.float32)),
        in_specs=[pl.BlockSpec(memory_space=pltpu.HBM)] * 2,
        out_specs=(vmem,) * 4,
        scratch_shapes=[
            big, big, big, big,
            pltpu.VMEM((1, 1, 128), jnp.float32),
            pltpu.VMEM((nx * ny, 1, 128), jnp.float32),
            pltpu.VMEM((2, 2 * by + by // 2, 128), jnp.float32),
            pltpu.VMEM((2, 2 * by + by // 2, 128), jnp.float32),
            dma((2,)), dma((2, 8)), dma((2, 8)),
            dma((1,)), dma((1,)), dma((2,)), dma((2,)),
        ],
        compiler_params=pltpu.CompilerParams(
            collective_id=0, has_side_effects=True, vmem_limit_bytes=24 * 2**20),
    )(*(pltpu.with_memory_space_constraint(a, pltpu.HBM) for a in (right_side, diagonal)))
    return pl.pallas_call(
        combine,
        out_shape=(block, block),
        in_specs=[vmem] * 5,
        out_specs=(pl.BlockSpec(memory_space=pl.ANY),) * 2,
        scratch_shapes=[
            pltpu.VMEM((bx, by, bz), jnp.float32),
            pltpu.VMEM((bx, by, bz), jnp.float32),
            dma((2, bx)),
        ],
        compiler_params=pltpu.CompilerParams(vmem_limit_bytes=24 * 2**20),
    )(right_side, f1, f2, f3, co)


def solution(mesh):
    placed = (P("gx", "gy", None), P("gx", "gy", None))
    return jax.shard_map(
        functools.partial(on_device, mesh.shape["gx"], mesh.shape["gy"]),
        mesh=mesh,
        in_specs=placed,
        out_specs=placed,
        check_vma=False,
    )
```

profile of v0, /device:TPU:0, one launch (start us, length us, event | category | flops | bytes accessed | tf_op | source)
XLA Modules:
  0.0 21.4 jit_solution(9867865796342531743)
XLA Ops:
  0.6 0.0 copy-start
  0.6 18.7 %shard_map.41 = (f32[16,64,192]{2,1,0:T(8,128)S(1)}, f32[16,64,192]{2,1,0:T(8,128)S(1)}, f32[16,64,192]{2,1,0:T(8,128)S(1)}, f32[8,128]{1,0:T(8,128)S(1)}) custom-call(f32[16,64,192]{2,1,0:T(8,128)} %f0_ref.1, f32[16,64,192]{2,1,0:T(8,128)} %d_ref.1), custom_call_target="tpu_custom_call" | custom-call | tf_op jit(solution)/shard_map/pallas_call | solution.py:397
  19.3 0.0 copy-done
  19.4 2.0 %shard_map.42 = (f32[16,64,192]{2,1,0:T(8,128)}, f32[16,64,192]{2,1,0:T(8,128)}) custom-call(f32[16,64,192]{2,1,0:T(8,128)S(1)} %copy-done, f32[16,64,192]{2,1,0:T(8,128)S(1)} %get-tuple-element.6.f1_ref, f32[16,64,192]{2,1,0:T(8,128)S(1)} %get-tuple-element.7.f2_ref, f32[16,64,192]{2,1,0:T(8,128)S(1)} %get-tuple-element.8.f3_ref, ...), custom_call_target="tpu_custom_call" | custom-call | tf_op jit(solution)/shard_map/pallas_call | solution.py:414
Async XLA Ops:
  0.6 18.7 %copy-start = (f32[16,64,192]{2,1,0:T(8,128)S(1)}, f32[16,64,192]{2,1,0:T(8,128)}, u32[]{:S(2)}) copy-start(f32[16,64,192]{2,1,0:T(8,128)} %f0_ref.1) | copy-start | bytes 2359300
where the time goes:
time: 21.5 us; the launch traced here: 21.4 us
  Pallas kernels  20.7 us (96%)
  between operations  0.65 us (3%)
    pallas_call x1, Pallas kernels, on_device(): pl.pallas_call(functools.partial(kernel, nx, ny), out_shape=(block, block...  18.7 us
    pallas_call x1, Pallas kernels, on_device(): pl.pallas_call(combine, out_shape=(block, block), in_specs=[vmem] * 5, ou...  2.03 us

commit v1 on v0

--- a/solution.py
+++ b/solution.py
@@ -95,9 +95,13 @@
     return solution_field + residual
 
 
+def stage_count(nx, ny):
+    return (max(nx, ny) - 1).bit_length()
+
+
 def kernel(nx, ny, b_ref, d_ref, v1_ref, v2_ref, v3_ref, co_ref,
            v0, dd, v1, v2, part, slots,
-           tail_out, tail_in, own_sem, send_sem, recv_sem, sum_send, sum_recv, tail_send, tail_recv):
+           tail_out, tail_in, own_sem, send_sem, recv_sem, sum_send, sum_recv, tail_send, tail_recv, ready):
     gx, gy = lax.axis_index("gx"), lax.axis_index("gy")
     bx, by, bz = b_ref.shape
     barrier = pltpu.get_barrier_semaphore()
@@ -110,28 +114,33 @@
                 ok = this if ok is None else ok & this
         return ok
 
-    def peer_x(k):
-        return lax.rem(gx + k, nx)
-
-    def peer_y(k):
-        return lax.rem(gy + k, ny)
-
     count = nx * ny
     me = gx * ny + gy
 
     def peer(k):
         to = lax.rem(me + k, count)
         return to // ny, lax.rem(to, ny)
-
-    @pl.loop(1, count)
-    def _(k):
-        pl.semaphore_signal(barrier, inc=1, device_id=peer(k), device_id_type=MESH)
 
     own = []
     for n, (src, dst) in enumerate(((b_ref, v0), (d_ref, dd))):
         own.append(pltpu.make_async_copy(
             src, dst.at[pl.ds(RIM, bx), pl.ds(ROWS, by), :], own_sem.at[n]))
         own[-1].start()
+
+    def greet(semaphore, reach):
+        for dx, dy in DIRS:
+            @pl.when(there(dx * reach, dy * reach))
+            def _(dx=dx, dy=dy):
+                pl.semaphore_signal(semaphore, inc=1, device_id=(gx + dx * reach, gy + dy * reach),
+                                    device_id_type=MESH)
+
+    def greeted(semaphore, reach):
+        def span(at, count):
+            return 1 + (at >= reach).astype(jnp.int32) + (at + reach < count).astype(jnp.int32)
+
+        pl.semaphore_wait(semaphore, span(gx, nx) * span(gy, ny) - 1)
+
+    greet(barrier, 1)
 
     @pl.when(gx == 0)
     def _():
@@ -204,7 +213,7 @@
         for array, layer, rows, to, lanes in tails(dx, False):
             array[layer, rows, last] = tail_in[side, to, lanes]
 
-    pl.semaphore_wait(barrier, count - 1)
+    greeted(barrier, 1)
 
     for n in range(2):
         for dx, dy in DIRS:
@@ -216,6 +225,20 @@
         @pl.when(there(dx, 0))
         def _(dx=dx):
             tail_copy(dx).start()
+
+    stages = stage_count(nx, ny)
+    entered = [0]
+
+    def enter():
+        if entered[0] > stages:
+            return
+        if entered[0]:
+            greeted(ready.at[entered[0] - 1], 2 ** (entered[0] - 1))
+        if entered[0] < stages:
+            greet(ready.at[entered[0]], 2 ** entered[0])
+        entered[0] += 1
+
+    enter()
 
     def arrived(directions):
         for n in range(2):
@@ -278,6 +301,7 @@
 
     sums = lax.fori_loop(RIM + 3, RIM + bx - 3, middle_rows, sums, unroll=2)
 
+    enter()
     arrived(DIRS[2:4])
     low_rows, high_rows = slice(0, 3 * ROWS), slice(by - ROWS, by + 2 * ROWS)
     low_in, high_in = gy > 0, gy < ny - 1
@@ -304,6 +328,7 @@
         return add_up(layer, slice(by, by + ROWS), f3, sums)
 
     sums = lax.fori_loop(RIM + 3, RIM + bx - 3, end_rows, sums, unroll=2)
+    enter()
     near_high = lax.rem(gx, 2) == 0
     for turn in range(2):
         high = near_high if turn == 0 else jnp.logical_not(near_high)
@@ -329,6 +354,8 @@
         starts = tuple(jnp.where(high, RIM + bx - 1 - k, RIM - 2 + k) for k in range(3))
         sums = stencils(starts, (3, 3, 3), inside, sums)
 
+    for _ in range(stages):
+        enter()
     lane = [jnp.sum(jnp.sum(s, 1, keepdims=True), 0, keepdims=True) for s in sums]
     lane_of = lax.broadcasted_iota(jnp.int32, (1, 128), 1)
     packed = jnp.zeros((1, 128), jnp.float32)
@@ -407,6 +434,7 @@
             pltpu.VMEM((2, 2 * by + by // 2, 128), jnp.float32),
             dma((2,)), dma((2, 8)), dma((2, 8)),
             dma((1,)), dma((1,)), dma((2,)), dma((2,)),
+            pltpu.SemaphoreType.REGULAR((stage_count(nx, ny),)),
         ],
         compiler_params=pltpu.CompilerParams(
             collective_id=0, has_side_effects=True, vmem_limit_bytes=24 * 2**20),

time: 21.5 us -> 21.3 us (level)
  no operation moved by 1% of the time
where the time goes in v1:
time: 21.3 us; the launch traced here: 21.2 us
  Pallas kernels  20.5 us (96%)
  between operations  0.65 us (3%)
    pallas_call x1, Pallas kernels, on_device(): pl.pallas_call(functools.partial(kernel, nx, ny), out_shape=(block, block...  18.5 us
    pallas_call x1, Pallas kernels, on_device(): pl.pallas_call(combine, out_shape=(block, block), in_specs=[vmem] * 5, ou...  2.03 us

profile of v1, /device:TPU:0, one launch (start us, length us, event | category | flops | bytes accessed | tf_op | source)
XLA Modules:
  0.0 21.2 jit_solution(17359918043019114162)
XLA Ops:
  0.6 0.0 copy-start
  0.6 18.5 %shard_map.41 = (f32[16,64,192]{2,1,0:T(8,128)S(1)}, f32[16,64,192]{2,1,0:T(8,128)S(1)}, f32[16,64,192]{2,1,0:T(8,128)S(1)}, f32[8,128]{1,0:T(8,128)S(1)}) custom-call(f32[16,64,192]{2,1,0:T(8,128)} %f0_ref.1, f32[16,64,192]{2,1,0:T(8,128)} %d_ref.1), custom_call_target="tpu_custom_call" | custom-call | tf_op jit(solution)/shard_map/pallas_call | solution.py:424
  19.1 0.0 copy-done
  19.1 2.0 %shard_map.42 = (f32[16,64,192]{2,1,0:T(8,128)}, f32[16,64,192]{2,1,0:T(8,128)}) custom-call(f32[16,64,192]{2,1,0:T(8,128)S(1)} %copy-done, f32[16,64,192]{2,1,0:T(8,128)S(1)} %get-tuple-element.6.f1_ref, f32[16,64,192]{2,1,0:T(8,128)S(1)} %get-tuple-element.7.f2_ref, f32[16,64,192]{2,1,0:T(8,128)S(1)} %get-tuple-element.8.f3_ref, ...), custom_call_target="tpu_custom_call" | custom-call | tf_op jit(solution)/shard_map/pallas_call | solution.py:442
Async XLA Ops:
  0.6 18.5 %copy-start = (f32[16,64,192]{2,1,0:T(8,128)S(1)}, f32[16,64,192]{2,1,0:T(8,128)}, u32[]{:S(2)}) copy-start(f32[16,64,192]{2,1,0:T(8,128)} %f0_ref.1) | copy-start | bytes 2359300

commit v2 on v1

v2 whole, which is shorter than its diff:
```python
import functools

import jax
import jax.numpy as jnp
from jax import lax
from jax.experimental import pallas as pl
from jax.experimental.pallas import tpu as pltpu
from jax.sharding import PartitionSpec as P

ITERS = 3
SHIFT = 6.0
MESH = pl.DeviceIdType.MESH
DIRS = ((1, 0), (-1, 0), (0, 1), (0, -1), (1, 1), (1, -1), (-1, 1), (-1, -1))
CORNERS = DIRS[4:]
ROWS = 8
LANES = 128
PIECE = 24


def stage_count(nx, ny):
    return (max(nx, ny) - 1).bit_length()


def coefficients(moments):
    def inner(f, g):
        total = None
        for i, a in enumerate(f):
            for j, c in enumerate(g):
                term = a * c * moments[i + j]
                total = term if total is None else total + term
        return total

    def times_a(f):
        out = [SHIFT * f[0]]
        for k in range(1, len(f)):
            out.append(SHIFT * f[k] + f[k - 1])
        return out + [f[-1]]

    def axpy(f, a, g):
        size = max(len(f), len(g))
        out = []
        for k in range(size):
            if k >= len(f):
                out.append(a * g[k])
            elif k >= len(g):
                out.append(f[k])
            else:
                out.append(f[k] + a * g[k])
        return out

    one = jnp.ones_like(moments[0])
    residual, solution_field = [one], []
    s_field, p_field = [], []
    for step in range(ITERS):
        w_field = times_a(residual)
        gamma = inner(residual, residual)
        delta = inner(w_field, residual)
        if step == 0:
            alpha = gamma / delta
            s_field, p_field = w_field, residual
        else:
            beta = gamma / gamma_prev
            alpha = gamma / (delta - beta * gamma / alpha_prev)
            s_field = axpy(w_field, beta, s_field)
            p_field = axpy(residual, beta, p_field)
        solution_field = axpy(solution_field, alpha, p_field)
        residual = axpy(residual, -alpha, s_field)
        gamma_prev, alpha_prev = gamma, alpha
    return solution_field + residual


def stage_count(nx, ny):
    return (max(nx, ny) - 1).bit_length()


def kernel(nx, ny, b_ref, d_ref, f0m, f0t, v1, v2, v3, co_ref,
           ddm, ddt, fym, fyt, dym, dyt, xs_up, xs_down, xr_low, xr_high, cs, cr, f2r, part, slots,
           own_sem, y_send, y_recv, x_send, x_recv, c_send, c_recv, f_send, f_recv, sum_send, sum_recv, ready):
    gx, gy = lax.axis_index("gx"), lax.axis_index("gy")
    bx, by, bz = b_ref.shape
    tail = bz - LANES
    barrier = pltpu.get_barrier_semaphore()
    own_rows = pl.ds(ROWS, by)
    own_layers = pl.ds(1, bx)
    tall = by + PIECE // 3

    def there(dx, dy):
        ok = None
        for at, step, count in ((gx, dx, nx), (gy, dy, ny)):
            if step:
                this = (at + step >= 0) & (at + step < count)
                ok = this if ok is None else ok & this
        return ok

    count = nx * ny
    me = gx * ny + gy
    low_x, high_x, low_y, high_y = gx > 0, gx < nx - 1, gy > 0, gy < ny - 1

    own = []
    for n, (src, main, end) in enumerate(((b_ref, f0m, f0t), (d_ref, ddm, ddt))):
        for m, (to, lanes) in enumerate(((main, pl.ds(0, LANES)), (end, pl.ds(LANES, tail)))):
            own.append(pltpu.make_async_copy(
                src.at[:, :, lanes], to.at[own_layers, own_rows, :], own_sem.at[2 * n + m]))
            own[-1].start()

    def greet(semaphore, reach):
        for dx, dy in DIRS:
            @pl.when(there(dx * reach, dy * reach))
            def _(dx=dx, dy=dy):
                pl.semaphore_signal(semaphore, inc=1, device_id=(gx + dx * reach, gy + dy * reach),
                                    device_id_type=MESH)

    def greeted(semaphore, reach):
        def span(at, size):
            return 1 + (at >= reach).astype(jnp.int32) + (at + reach < size).astype(jnp.int32)

        pl.semaphore_wait(semaphore, span(gx, nx) * span(gy, ny) - 1)

    greet(barrier, 1)

    def clear(ref):
        ref[...] = jnp.zeros(ref.shape, jnp.float32)

    for k in (0, bx - 2, bx - 1):
        for row in (ROWS - 1, ROWS + by):
            f0m[k + 1, row:row + 1] = jnp.zeros((1, LANES), jnp.float32)
            f0t[k + 1, row:row + 1] = jnp.zeros((1, tail), jnp.float32)
    for side, ok in enumerate((low_y, high_y)):
        @pl.when(jnp.logical_not(ok))
        def _(side=side):
            for ref in (fym, fyt, dym, dyt):
                clear(ref.at[side])
    for ref, ok in ((xr_low, low_x), (xr_high, high_x)):
        @pl.when(jnp.logical_not(ok))
        def _(ref=ref):
            clear(ref)
    for c, (dx, dy) in enumerate(CORNERS):
        @pl.when(jnp.logical_not(there(-dx, -dy)))
        def _(c=c):
            clear(cr.at[c])

    lane = lax.broadcasted_iota(jnp.int32, (PIECE, LANES), 1)
    row = lax.broadcasted_iota(jnp.int32, (PIECE, LANES), 0)

    def rolled(x, by_lanes):
        return pltpu.roll(x, by_lanes, axis=1)

    def widen(x):
        return jnp.concatenate([x, jnp.zeros((x.shape[0], LANES - tail), jnp.float32)], 1)

    def f0(t, layer, start, size):
        rows = pl.ds(start, size)
        return widen(f0t[layer, rows]) if t else f0m[layer, rows]

    def dd(t, layer, start, size):
        rows = pl.ds(start, size)
        return widen(ddt[layer, rows]) if t else ddm[layer, rows]

    def g1(t, layer, start, size):
        return v1[t, layer, pl.ds(start, size)]

    def g2(t, layer, start, size):
        return v2[t, layer, pl.ds(start, size)]

    def beside_z(a, b):
        at = lane[:a.shape[0]]
        left_a, left_b = rolled(a, 1), rolled(b, 1)
        right_a, right_b = rolled(a, LANES - 1), rolled(b, LANES - 1)
        return (jnp.where(at == 0, left_b, left_a) + jnp.where(at == LANES - 1, right_b, right_a),
                jnp.where(at == 0, left_a, left_b) + right_b)

    def times_b(shift, here, others):
        z = beside_z(*here)
        out = []
        for t in range(2):
            total = z[t]
            for o in others:
                total = total + o[t]
            out.append(shift[t] * here[t] - total)
        out[1] = jnp.where(lane[:out[1].shape[0]] < tail, out[1], 0.0)
        return out

    def apply(field, layer, start, size, steps, edges=()):
        two = range(2)
        here = [field(t, layer, start, size) for t in two]
        others = [[field(t, layer, start + step, size) for t in two] for step in (-1, 1)]
        others += [[field(t, layer + step, start, size) for t in two] for step in steps]
        out = times_b([dd(t, layer, start, size) for t in two], here, others)
        if edges:
            at = row + start
            if start < ROWS:
                ok = (at >= ROWS) | low_y
                out = [jnp.where(ok, o, 0.0) for o in out]
            if start + size > ROWS + by:
                ok = (at < ROWS + by) | high_y
                out = [jnp.where(ok, o, 0.0) for o in out]
        return out

    def tall_apply(field, to, layer, first, steps=(-1, 1)):
        for start in range(first, first + tall, PIECE):
            out = apply(field, layer, start, PIECE, steps, True)
            for t in range(2):
                to[t, layer, pl.ds(start, PIECE)] = out[t]

    def halves(a, b):
        return jnp.where(lax.broadcasted_iota(jnp.int32, a.shape, 1) < tail, a, rolled(b, tail))

    for copy in own:
        copy.wait()

    for k, steps, buffer in ((bx - 1, (-1,), xs_up), (0, (1,), xs_down)):
        for start in range(0, by, 16):
            rows = slice(start, start + 16)
            field = [f0(t, k + 1, ROWS + start, 16) for t in range(2)]
            partial = apply(f0, k + 1, ROWS + start, 16, steps)
            buffer[0, rows], buffer[1, rows] = field[0], partial[0]
            buffer[2, rows] = halves(field[1], partial[1])
    for start in range(0, by, 16):
        rows = slice(start, start + 16)
        shift = [dd(t, bx, ROWS + start, 16) for t in range(2)]
        partial = apply(f0, bx - 1, ROWS + start, 16, (-1, 1))
        xs_up[3, rows], xs_up[4, rows] = shift[0], partial[0]
        xs_up[5, rows] = halves(shift[1], partial[1])
    for c, (dx, dy) in enumerate(CORNERS):
        edge, second = (bx, bx - 1) if dx > 0 else (1, 2)
        first, near = (ROWS + by - 2, ROWS + by - 1) if dy > 0 else (ROWS, ROWS)
        cs[c, 0:2] = f0m[edge, first:first + 2]
        cs[c, 2:3] = f0m[second, near:near + 1]
        cs[c, 3:4] = ddm[edge, near:near + 1]
        cs[c, 4:6, 0:tail] = f0t[edge, first:first + 2]
        cs[c, 6:7, 0:tail] = f0t[second, near:near + 1]
        cs[c, 7:8, 0:tail] = ddt[edge, near:near + 1]

    def y_copies(dy):
        side = 0 if dy > 0 else 1
        out = []
        for n, (src, dst, width) in enumerate(((f0m, fym, 3), (f0t, fyt, 3), (ddm, dym, 2), (ddt, dyt, 2))):
            first = ROWS + by - width if dy > 0 else ROWS
            out.append(pltpu.make_async_remote_copy(
                src_ref=src.at[own_layers, pl.ds(first, width), :], dst_ref=dst.at[side],
                send_sem=y_send.at[side, n], recv_sem=y_recv.at[side, n],
                device_id=(gx, gy + dy), device_id_type=MESH))
        return out

    def x_copies(dx):
        if dx > 0:
            pieces = ((xs_up.at[pl.ds(0, 3)], xr_low.at[pl.ds(0, 3)], 0),
                      (xs_up.at[pl.ds(3, 3)], xr_low.at[pl.ds(3, 3)], 1))
        else:
            pieces = ((xs_down, xr_high, 2),)
        return [pltpu.make_async_remote_copy(
            src_ref=src, dst_ref=dst, send_sem=x_send.at[n], recv_sem=x_recv.at[n],
            device_id=(gx + dx, gy), device_id_type=MESH) for src, dst, n in pieces]

    def c_copy(c):
        dx, dy = CORNERS[c]
        return [pltpu.make_async_remote_copy(
            src_ref=cs.at[c], dst_ref=cr.at[c], send_sem=c_send.at[c], recv_sem=c_recv.at[c],
            device_id=(gx + dx, gy + dy), device_id_type=MESH)]

    def f2_copy():
        return [pltpu.make_async_remote_copy(
            src_ref=v2.at[:, 1, own_rows, :], dst_ref=f2r, send_sem=f_send.at[0], recv_sem=f_recv.at[0],
            device_id=(gx - 1, gy), device_id_type=MESH)]

    def every(make, at, what):
        @pl.when(at)
        def _():
            for copy in make():
                getattr(copy, what)()

    x_makes = [(functools.partial(x_copies, dx), (dx, 0)) for dx in (1, -1)]
    y_makes = [(functools.partial(y_copies, dy), (0, dy)) for dy in (1, -1)]
    c_makes = [(functools.partial(c_copy, c), CORNERS[c]) for c in range(4)]

    greeted(barrier, 1)
    for make, (dx, dy) in x_makes + y_makes + c_makes:
        every(make, there(dx, dy), "start")

    def arrived(makes):
        for make, (dx, dy) in makes:
            every(make, there(-dx, -dy), "wait_recv")

    stages = stage_count(nx, ny)
    entered = [0]

    def enter():
        if entered[0] > stages:
            return
        if entered[0]:
            greeted(ready.at[entered[0] - 1], 2 ** (entered[0] - 1))
        if entered[0] < stages:
            greet(ready.at[entered[0]], 2 ** entered[0])
        entered[0] += 1

    enter()

    sums = [jnp.zeros((8, LANES), jnp.float32)] * 6

    def add(n, a, b):
        total = sums[n]
        for t in range(2):
            product = a[t] * b[t]
            for g in range(product.shape[0] // 8):
                total = total + product[8 * g:8 * g + 8]
        sums[n] = total

    def moments(k, which):
        layer = k + 1
        for start in range(ROWS, ROWS + by, 16):
            fields = {}

            def get(n):
                if n not in fields:
                    fields[n] = [(f0, g1, g2)[n](t, layer, start, 16) for t in range(2)]
                return fields[n]

            for n in which:
                if n < 5:
                    add(n, get(n // 2), get((n + 1) // 2))
                else:
                    a, b = get(2)
                    at = lane[:16]
                    left_a, left_b = rolled(a, 1), rolled(b, 1)
                    z = (jnp.where(at == 0, left_b, left_a), jnp.where(at == 0, left_a, left_b))
                    value = []
                    for t in range(2):
                        other = z[t] + g2(t, layer, start - 1, 16) + g2(t, layer - 1, start, 16)
                        value.append(dd(t, layer, start, 16) * get(2)[t] - (other + other))
                    value[1] = jnp.where(at < tail, value[1], 0.0)
                    add(5, get(2), value)

    for k in range(bx):
        moments(k, (0,))
    enter()

    arrived(y_makes)
    enter()
    for ref, small, width in ((f0m, fym, 3), (f0t, fyt, 3), (ddm, dym, 2), (ddt, dyt, 2)):
        ref[1:bx + 1, ROWS - width:ROWS] = small[0]
        ref[1:bx + 1, ROWS + by:ROWS + by + width] = small[1]

    first1, first2 = ROWS - 2, ROWS - 1
    for k in range(bx):
        steps = (1,) if k == 0 else (-1,) if k == bx - 1 else (-1, 1)
        tall_apply(f0, v1, k + 1, first1, steps)
    for k in range(1, bx - 1):
        steps = (1,) if k == 1 else (-1,) if k == bx - 2 else (-1, 1)
        tall_apply(g1, v2, k + 1, first2, steps)
        moments(k, (1, 2))
    for k in range(2, bx - 2):
        moments(k, (3, 4) + ((5,) if k > 2 else ()))

    arrived(x_makes + c_makes)
    for dx in (1, -1):
        got = xr_low if dx > 0 else xr_high
        halo, edge = (0, 1) if dx > 0 else (bx + 1, bx)
        ok = low_x if dx > 0 else high_x
        f0m[halo, ROWS:ROWS + by] = got[0]
        f0t[halo, ROWS:ROWS + by] = got[2][:, :tail]
        corner = [CORNERS.index((dx, dy)) for dy in (1, -1)]
        for c, first in zip(corner, (ROWS - 2, ROWS + by)):
            f0m[halo, first:first + 2] = cr[c, 0:2]
            f0t[halo, first:first + 2] = cr[c, 4:6, 0:tail]
        for start in range(0, by, 16):
            rows = slice(start, start + 16)
            within = (got[1, rows], rolled(got[2, rows], LANES - tail))
            for t in range(2):
                value = within[t] - f0(t, edge, ROWS + start, 16)
                if t:
                    value = jnp.where(lane[:16] < tail, value, 0.0)
                for at, beyond in ((0, -1), (by - 16, 1)):
                    if start == at:
                        where = row[:16] == (0 if beyond < 0 else 15)
                        value = value - jnp.where(where, f0(t, halo, ROWS + start + beyond, 16), 0.0)
                v1[t, halo, pl.ds(ROWS + start, 16)] = jnp.where(ok, value, 0.0)
        for c, at, y_ok in zip(corner, (ROWS - 1, ROWS + by), (low_y, high_y)):
            two = range(2)
            here = [f0(t, halo, at, 1) for t in two]
            others = [[f0(t, halo, at + step, 1) for t in two] for step in (-1, 1)]
            others.append([f0(t, edge, at, 1) for t in two])
            pick = lambda n: [cr[c, n:n + 1], widen(cr[c, n + 4:n + 5, 0:tail])]
            others.append(pick(2))
            out = times_b(pick(3), here, others)
            for t in two:
                v1[t, halo, at:at + 1] = jnp.where(ok & y_ok, out[t], 0.0)
        for start in range(first1, first1 + tall, PIECE):
            for t in range(2):
                v1[t, edge, pl.ds(start, PIECE)] = g1(t, edge, start, PIECE) - f0(t, halo, start, PIECE)
        inner = edge + dx
        tall_apply(g1, v2, edge, first2)
        for start in range(first2, first2 + tall, PIECE):
            for t in range(2):
                v2[t, inner, pl.ds(start, PIECE)] = g2(t, inner, start, PIECE) - g1(t, edge, start, PIECE)
        if dx > 0:
            for start in range(0, by, 16):
                rows, at = slice(start, start + 16), ROWS + start
                two = range(2)
                here = [g1(t, 0, at, 16) for t in two]
                others = [[g1(t, 0, at + step, 16) for t in two] for step in (-1, 1)]
                others.append([g1(t, 1, at, 16) for t in two])
                others.append([got[4, rows], rolled(got[5, rows], LANES - tail)])
                out = times_b([got[3, rows], got[5, rows]], here, others)
                for t in two:
                    value = out[t]
                    for c, where in zip(corner, (0, by - 1)):
                        if start <= where < start + 16:
                            far = widen(cr[c, 6:7, 0:tail]) if t else cr[c, 2:3]
                            value = value + jnp.where(row[:16] == where - start, far, 0.0)
                    v2[t, 0, pl.ds(at, 16)] = jnp.where(low_x, value, 0.0)
            moments(0, (1, 2, 3, 4, 5))
            moments(1, (3, 4, 5))
            moments(2, (5,))
        else:
            moments(bx - 2, (3, 4, 5))
            moments(bx - 1, (1, 2, 3, 4, 5))

    for _ in range(stages):
        enter()
    lane_of = lax.broadcasted_iota(jnp.int32, (8, LANES), 1)
    row_of = lax.broadcasted_iota(jnp.int32, (8, LANES), 0)
    stacked = jnp.zeros((8, LANES), jnp.float32)
    for n, s in enumerate(sums):
        stacked = jnp.where(row_of == n, jnp.sum(s, 0, keepdims=True), stacked)
    packed = jnp.sum(jnp.where(lane_of == row_of, jnp.sum(stacked, 1, keepdims=True), 0.0), 0, keepdims=True)
    part[0] = packed

    def wrapped(at, size):
        return jnp.where(at >= size, at - size, at)

    @pl.loop(0, nx, unroll=nx * ny <= 64)
    def _(i):
        x = wrapped(nx - 1 - gx + i, nx)

        @pl.loop(0, ny, unroll=nx * ny <= 64)
        def _(j):
            y = wrapped(ny - 1 - gy + j, ny)

            @pl.when((x != gx) | (y != gy))
            def _():
                pltpu.make_async_remote_copy(
                    src_ref=part.at[0], dst_ref=slots.at[me], send_sem=sum_send.at[0],
                    recv_sem=sum_recv.at[0], device_id=(x, y), device_id_type=MESH).start()

    every(f2_copy, low_x, "start")
    slots[me] = packed

    for k in range(bx):
        layer = k + 1
        for start in range(ROWS, ROWS + by, 16):
            out = apply(g2, layer, start, 16, (-1, 1) if k < bx - 1 else (-1,))
            for t in range(2):
                v3[t, k, pl.ds(start - ROWS, 16)] = out[t]

    @pl.when(high_x)
    def _():
        for copy in f2_copy():
            copy.wait_recv()
        for t in range(2):
            v3[t, bx - 1] = v3[t, bx - 1] - f2r[t]

    others = slots.at[pl.ds(0, count - 1)]
    pltpu.make_async_copy(others, others, sum_recv.at[0]).wait()
    total = jnp.sum(slots[...], 0)
    moment = [total[:, k:k + 1] for k in range(6)]
    co = jnp.zeros((8, LANES), jnp.float32)
    for k, c in enumerate(coefficients(moment)):
        co = jnp.where(row_of == k, c, co)
    co_ref[...] = co
    pltpu.make_async_copy(others, others, sum_send.at[0]).wait()
    for make, (dx, dy) in x_makes + y_makes + c_makes:
        every(make, there(dx, dy), "wait_send")
    every(f2_copy, low_x, "wait_send")


def combine(f0m, f0t, v1, v2, v3, co_ref, x_out, r_out, x_buf, r_buf, sems):
    bx, by, bz = x_out.shape
    tail = bz - LANES
    c = [jnp.broadcast_to(co_ref[k:k + 1, :], (by, LANES)) for k in range(7)]
    rows = pl.ds(ROWS, by)

    def copy(n, k):
        src, dst = ((x_buf, x_out), (r_buf, r_out))[n]
        return pltpu.make_async_copy(src.at[pl.ds(k, 1)], dst.at[pl.ds(k, 1)], sems.at[n, k])

    for k in range(bx):
        for t in range(2):
            wide = LANES if t == 0 else tail
            lanes = slice(LANES * t, LANES * t + wide)
            f0 = f0t[k + 1, rows] if t else f0m[k + 1, rows]
            f1, f2, f3 = (v1[t, k + 1, rows], v2[t, k + 1, rows], v3[t, k])
            m = [a[:, :wide] for a in c]
            f1, f2, f3 = f1[:, :wide], f2[:, :wide], f3[:, :wide]
            x_buf[k, :, lanes] = m[0] * f0 + m[1] * f1 + m[2] * f2
            r_buf[k, :, lanes] = m[3] * f0 + m[4] * f1 + m[5] * f2 + m[6] * f3
        for n in range(2):
            copy(n, k).start()
    for k in range(bx):
        for n in range(2):
            copy(n, k).wait()


def on_device(nx, ny, right_side, diagonal):
    bx, by, bz = right_side.shape
    tail = bz - LANES
    f32 = jnp.float32
    block = jax.ShapeDtypeStruct((bx, by, bz), f32)
    high, deep = bx + 2, by + 2 * ROWS
    vmem = pl.BlockSpec(memory_space=pltpu.VMEM)
    dma = pltpu.SemaphoreType.DMA
    shape = lambda *dims: jax.ShapeDtypeStruct(dims, f32)
    space = lambda *dims: pltpu.VMEM(dims, f32)
    fields = pl.pallas_call(
        functools.partial(kernel, nx, ny),
        out_shape=(shape(high, deep, LANES), shape(high, deep, tail), shape(2, high, deep, LANES),
                   shape(2, high, deep, LANES), shape(2, bx, by, LANES), shape(8, LANES)),
        in_specs=[pl.BlockSpec(memory_space=pltpu.HBM)] * 2,
        out_specs=(vmem,) * 6,
        scratch_shapes=[
            space(high, deep, LANES), space(high, deep, tail),
            space(2, bx, 3, LANES), space(2, bx, 3, tail), space(2, bx, 2, LANES), space(2, bx, 2, tail),
            space(6, by, LANES), space(3, by, LANES), space(6, by, LANES), space(3, by, LANES),
            space(4, 8, LANES), space(4, 8, LANES), space(2, by, LANES),
            space(1, 1, LANES), space(nx * ny, 1, LANES),
            dma((4,)), dma((2, 4)), dma((2, 4)), dma((3,)), dma((3,)), dma((4,)), dma((4,)),
            dma((1,)), dma((1,)), dma((1,)), dma((1,)),
            pltpu.SemaphoreType.REGULAR((stage_count(nx, ny),)),
        ],
        compiler_params=pltpu.CompilerParams(
            collective_id=0, has_side_effects=True, vmem_limit_bytes=32 * 2**20),
    )(*(pltpu.with_memory_space_constraint(a, pltpu.HBM) for a in (right_side, diagonal)))
    return pl.pallas_call(
        combine,
        out_shape=(block, block),
        in_specs=[vmem] * 6,
        out_specs=(pl.BlockSpec(memory_space=pl.ANY),) * 2,
        scratch_shapes=[space(bx, by, bz), space(bx, by, bz), dma((2, bx))],
        compiler_params=pltpu.CompilerParams(vmem_limit_bytes=24 * 2**20),
    )(*fields)


def solution(mesh):
    placed = (P("gx", "gy", None), P("gx", "gy", None))
    return jax.shard_map(
        functools.partial(on_device, mesh.shape["gx"], mesh.shape["gy"]),
        mesh=mesh,
        in_specs=placed,
        out_specs=placed,
        check_vma=False,
    )
```

time: 21.3 us -> 18.8 us (0.88)
  Pallas kernels: 20.5 us -> 18 us
    pallas_call x2, Pallas kernels: 20.5 us -> 18 us  [the longest x1 16.4 us: on_device(): pl.pallas_call(functools.partial(kernel, nx, ny), out_shape=(shape(high,...]
where the time goes in v2:
time: 18.8 us; the launch traced here: 18.6 us
  Pallas kernels  18 us (96%)
  between operations  0.64 us (3%)
    pallas_call x1, Pallas kernels, on_device(): pl.pallas_call(functools.partial(kernel, nx, ny), out_shape=(shape(high,...  16.4 us
    pallas_call x1, Pallas kernels, on_device(): pl.pallas_call(combine, out_shape=(block, block), in_specs=[vmem] * 6, ou...  1.59 us

profile of v2, /device:TPU:0, one launch (start us, length us, event | category | flops | bytes accessed | tf_op | source)
XLA Modules:
  0.0 18.6 jit_solution(2044275200997855816)
XLA Ops:
  0.6 16.4 %shard_map.41 = (f32[18,80,128]{2,1,0:T(8,128)S(1)}, f32[18,80,64]{2,1,0:T(8,128)S(1)}, f32[2,18,80,128]{3,2,1,0:T(8,128)S(1)}, f32[2,18,80,128]{3,2,1,0:T(8,128...) custom-call(f32[16,64,192]{2,1,0:T(8,128)} %b_ref.1, f32[16,64,192]{2,1,0:T(8,128)} %d_ref.1), custom_call_target="tpu_custom_call" | custom-call | tf_op jit(solution)/shard_map/pallas_call | solution.py:513
  17.0 1.6 %shard_map.42 = (f32[16,64,192]{2,1,0:T(8,128)}, f32[16,64,192]{2,1,0:T(8,128)}) custom-call(f32[18,80,128]{2,1,0:T(8,128)S(1)} %get-tuple-element.8.f0m, f32[18,80,64]{2,1,0:T(8,128)S(1)} %get-tuple-element.9.f0t, f32[2,18,80,128]{3,2,1,0:T(8,128)S(1)} %get-tuple-element.10.v1, f32[2,18,80,128]{3,2,1,0:T(8,128)S(1)} %get-tuple-element.11.v2, ...), custom_call_target="tpu_custom_call" | custom-call | tf_op jit(solution)/shard_map/pallas_call | solution.py:532

commit v3 on v2

--- a/solution.py
+++ b/solution.py
@@ -7,7 +7,6 @@
 from jax.experimental.pallas import tpu as pltpu
 from jax.sharding import PartitionSpec as P
 
-ITERS = 3
 SHIFT = 6.0
 MESH = pl.DeviceIdType.MESH
 DIRS = ((1, 0), (-1, 0), (0, 1), (0, -1), (1, 1), (1, -1), (-1, 1), (-1, -1))
@@ -21,56 +20,18 @@
     return (max(nx, ny) - 1).bit_length()
 
 
-def coefficients(moments):
-    def inner(f, g):
-        total = None
-        for i, a in enumerate(f):
-            for j, c in enumerate(g):
-                term = a * c * moments[i + j]
-                total = term if total is None else total + term
-        return total
-
-    def times_a(f):
-        out = [SHIFT * f[0]]
-        for k in range(1, len(f)):
-            out.append(SHIFT * f[k] + f[k - 1])
-        return out + [f[-1]]
-
-    def axpy(f, a, g):
-        size = max(len(f), len(g))
-        out = []
-        for k in range(size):
-            if k >= len(f):
-                out.append(a * g[k])
-            elif k >= len(g):
-                out.append(f[k])
-            else:
-                out.append(f[k] + a * g[k])
-        return out
-
-    one = jnp.ones_like(moments[0])
-    residual, solution_field = [one], []
-    s_field, p_field = [], []
-    for step in range(ITERS):
-        w_field = times_a(residual)
-        gamma = inner(residual, residual)
-        delta = inner(w_field, residual)
-        if step == 0:
-            alpha = gamma / delta
-            s_field, p_field = w_field, residual
-        else:
-            beta = gamma / gamma_prev
-            alpha = gamma / (delta - beta * gamma / alpha_prev)
-            s_field = axpy(w_field, beta, s_field)
-            p_field = axpy(residual, beta, p_field)
-        solution_field = axpy(solution_field, alpha, p_field)
-        residual = axpy(residual, -alpha, s_field)
-        gamma_prev, alpha_prev = gamma, alpha
-    return solution_field + residual
-
-
-def stage_count(nx, ny):
-    return (max(nx, ny) - 1).bit_length()
+def coefficients(m):
+    a = [m[k + 1] + SHIFT * m[k] for k in range(5)]
+    inverse0 = 1.0 / a[0]
+    lower1, lower2 = a[1] * inverse0, a[2] * inverse0
+    inverse1 = 1.0 / (a[2] - a[1] * lower1)
+    across = a[3] - a[2] * lower1
+    right1, right2 = m[1] - m[0] * lower1, m[2] - m[0] * lower2
+    lower3 = across * inverse1
+    x2 = (right2 - right1 * lower3) / (a[4] - a[2] * lower2 - across * lower3)
+    x1 = (right1 - across * x2) * inverse1
+    x0 = (m[0] - a[1] * x1 - a[2] * x2) * inverse0
+    return x0, x1, x2, 1.0 - SHIFT * x0, -SHIFT * x1 - x0, -SHIFT * x2 - x1, -x2
 
 
 def kernel(nx, ny, b_ref, d_ref, f0m, f0t, v1, v2, v3, co_ref,
@@ -96,27 +57,27 @@
     me = gx * ny + gy
     low_x, high_x, low_y, high_y = gx > 0, gx < nx - 1, gy > 0, gy < ny - 1
 
+    def greet(semaphore, reach):
+        for dx, dy in DIRS:
+            @pl.when(there(dx * reach, dy * reach))
+            def _(dx=dx, dy=dy):
+                pl.semaphore_signal(semaphore, inc=1, device_id=(gx + dx * reach, gy + dy * reach),
+                                    device_id_type=MESH)
+
+    def greeted(semaphore, reach):
+        def span(at, size):
+            return 1 + (at >= reach).astype(jnp.int32) + (at + reach < size).astype(jnp.int32)
+
+        pl.semaphore_wait(semaphore, span(gx, nx) * span(gy, ny) - 1)
+
+    greet(barrier, 1)
+
     own = []
     for n, (src, main, end) in enumerate(((b_ref, f0m, f0t), (d_ref, ddm, ddt))):
         for m, (to, lanes) in enumerate(((main, pl.ds(0, LANES)), (end, pl.ds(LANES, tail)))):
             own.append(pltpu.make_async_copy(
                 src.at[:, :, lanes], to.at[own_layers, own_rows, :], own_sem.at[2 * n + m]))
             own[-1].start()
-
-    def greet(semaphore, reach):
-        for dx, dy in DIRS:
-            @pl.when(there(dx * reach, dy * reach))
-            def _(dx=dx, dy=dy):
-                pl.semaphore_signal(semaphore, inc=1, device_id=(gx + dx * reach, gy + dy * reach),
-                                    device_id_type=MESH)
-
-    def greeted(semaphore, reach):
-        def span(at, size):
-            return 1 + (at >= reach).astype(jnp.int32) + (at + reach < size).astype(jnp.int32)
-
-        pl.semaphore_wait(semaphore, span(gx, nx) * span(gy, ny) - 1)
-
-    greet(barrier, 1)
 
     def clear(ref):
         ref[...] = jnp.zeros(ref.shape, jnp.float32)
@@ -425,17 +386,10 @@
     packed = jnp.sum(jnp.where(lane_of == row_of, jnp.sum(stacked, 1, keepdims=True), 0.0), 0, keepdims=True)
     part[0] = packed
 
-    def wrapped(at, size):
-        return jnp.where(at >= size, at - size, at)
-
     @pl.loop(0, nx, unroll=nx * ny <= 64)
-    def _(i):
-        x = wrapped(nx - 1 - gx + i, nx)
-
+    def _(x):
         @pl.loop(0, ny, unroll=nx * ny <= 64)
-        def _(j):
-            y = wrapped(ny - 1 - gy + j, ny)
-
+        def _(y):
             @pl.when((x != gx) | (y != gy))
             def _():
                 pltpu.make_async_remote_copy(
@@ -459,18 +413,18 @@
         for t in range(2):
             v3[t, bx - 1] = v3[t, bx - 1] - f2r[t]
 
+    for make, (dx, dy) in x_makes + y_makes + c_makes:
+        every(make, there(dx, dy), "wait_send")
+    every(f2_copy, low_x, "wait_send")
     others = slots.at[pl.ds(0, count - 1)]
+    pltpu.make_async_copy(others, others, sum_send.at[0]).wait()
     pltpu.make_async_copy(others, others, sum_recv.at[0]).wait()
     total = jnp.sum(slots[...], 0)
-    moment = [total[:, k:k + 1] for k in range(6)]
+    moment = [jnp.broadcast_to(total[:, k:k + 1], (1, LANES)) for k in range(6)]
     co = jnp.zeros((8, LANES), jnp.float32)
     for k, c in enumerate(coefficients(moment)):
         co = jnp.where(row_of == k, c, co)
     co_ref[...] = co
-    pltpu.make_async_copy(others, others, sum_send.at[0]).wait()
-    for make, (dx, dy) in x_makes + y_makes + c_makes:
-        every(make, there(dx, dy), "wait_send")
-    every(f2_copy, low_x, "wait_send")
 
 
 def combine(f0m, f0t, v1, v2, v3, co_ref, x_out, r_out, x_buf, r_buf, sems):

time: 18.8 us -> 18.5 us (0.984)
  Pallas kernels: 18 us -> 17.8 us
    pallas_call x1, Pallas kernels: 16.4 us -> 16.2 us  [on_device(): pl.pallas_call(functools.partial(kernel, nx, ny), out_shape=(shape(high,...]
where the time goes in v3:
time: 18.5 us; the launch traced here: 18.4 us
  Pallas kernels  17.8 us (96%)
  between operations  0.64 us (3%)
    pallas_call x1, Pallas kernels, on_device(): pl.pallas_call(functools.partial(kernel, nx, ny), out_shape=(shape(high,...  16.2 us
    pallas_call x1, Pallas kernels, on_device(): pl.pallas_call(combine, out_shape=(block, block), in_specs=[vmem] * 6, ou...  1.59 us

profile of v3, /device:TPU:0, one launch (start us, length us, event | category | flops | bytes accessed | tf_op | source)
XLA Modules:
  0.0 18.4 jit_solution(4361557273908999696)
XLA Ops:
  0.6 16.2 %shard_map.41 = (f32[18,80,128]{2,1,0:T(8,128)S(1)}, f32[18,80,64]{2,1,0:T(8,128)S(1)}, f32[2,18,80,128]{3,2,1,0:T(8,128)S(1)}, f32[2,18,80,128]{3,2,1,0:T(8,128...) custom-call(f32[16,64,192]{2,1,0:T(8,128)} %b_ref.1, f32[16,64,192]{2,1,0:T(8,128)} %d_ref.1), custom_call_target="tpu_custom_call" | custom-call | tf_op jit(solution)/shard_map/pallas_call | solution.py:467
  16.8 1.6 %shard_map.42 = (f32[16,64,192]{2,1,0:T(8,128)}, f32[16,64,192]{2,1,0:T(8,128)}) custom-call(f32[18,80,128]{2,1,0:T(8,128)S(1)} %get-tuple-element.8.f0m, f32[18,80,64]{2,1,0:T(8,128)S(1)} %get-tuple-element.9.f0t, f32[2,18,80,128]{3,2,1,0:T(8,128)S(1)} %get-tuple-element.10.v1, f32[2,18,80,128]{3,2,1,0:T(8,128)S(1)} %get-tuple-element.11.v2, ...), custom_call_target="tpu_custom_call" | custom-call | tf_op jit(solution)/shard_map/pallas_call | solution.py:486

commit v4 on v3

v4 whole, which is shorter than its diff:
```python
import functools

import jax
import jax.numpy as jnp
from jax import lax
from jax.experimental import pallas as pl
from jax.experimental.pallas import tpu as pltpu
from jax.sharding import PartitionSpec as P

SHIFT = 6.0
MESH = pl.DeviceIdType.MESH
DIRS = ((1, 0), (-1, 0), (0, 1), (0, -1), (1, 1), (1, -1), (-1, 1), (-1, -1))
CORNERS = ((1, 1), (-1, -1), (1, -1), (-1, 1))
ROWS = 8
LANES = 128
CHUNK = 16


def relay_reaches(ny):
    return [2 ** n for n in range((ny - 1).bit_length())]


def coefficients(m):
    a = [m[k + 1] + SHIFT * m[k] for k in range(5)]
    inverse0 = 1.0 / a[0]
    lower1, lower2 = a[1] * inverse0, a[2] * inverse0
    inverse1 = 1.0 / (a[2] - a[1] * lower1)
    across = a[3] - a[2] * lower1
    right1, right2 = m[1] - m[0] * lower1, m[2] - m[0] * lower2
    lower3 = across * inverse1
    x2 = (right2 - right1 * lower3) / (a[4] - a[2] * lower2 - across * lower3)
    x1 = (right1 - across * x2) * inverse1
    x0 = (m[0] - a[1] * x1 - a[2] * x2) * inverse0
    return x0, x1, x2, 1.0 - SHIFT * x0, -SHIFT * x1 - x0, -SHIFT * x2 - x1, -x2


def kernel(nx, ny, b_ref, d_ref, f0m, f0t, v1, v2, v3, co_ref,
           ddm, ddt, xs, xr, ys, yr, cs, cr, ex, ey, hy, fx, fy, fys, fyr, part, slots,
           own_sem, x_send, x_recv, y_send, y_recv, c_send, c_recv,
           fx_send, fx_recv, fy_send, fy_recv, sum_send, sum_recv, ready):
    gx, gy = lax.axis_index("gx"), lax.axis_index("gy")
    bx, by, bz = b_ref.shape
    tail = bz - LANES
    high, deep = f0m.shape[:2]
    two = range(2)
    barrier = pltpu.get_barrier_semaphore()
    count = nx * ny
    me = gx * ny + gy
    x_ok, y_ok = (gx > 0, gx < nx - 1), (gy > 0, gy < ny - 1)
    x_count, y_count = (sum(o.astype(jnp.int32) for o in ok) for ok in (x_ok, y_ok))
    first, last = ROWS, ROWS + by - 1
    x_side = ((0, 1, 2), (bx + 1, bx, bx - 1))
    y_side = ((first - 1, first, first + 1), (last + 1, last, last - 1))
    x_half, y_half = by // 2, bx // 2

    def there(dx, dy):
        ok = None
        for at, step, size in ((gx, dx, nx), (gy, dy, ny)):
            if step:
                this = (at + step >= 0) & (at + step < size)
                ok = this if ok is None else ok & this
        return ok

    def greet(semaphore, reach):
        for dy in (reach, -reach):
            @pl.when(there(0, dy))
            def _(dy=dy):
                pl.semaphore_signal(semaphore, inc=1, device_id=(gx, gy + dy), device_id_type=MESH)

    def greeted(semaphore, reach, more=0):
        present = (gy >= reach).astype(jnp.int32) + (gy + reach < ny).astype(jnp.int32)
        pl.semaphore_wait(semaphore, present + more)

    @pl.loop(0, nx, unroll=nx <= 16)
    def _(x):
        @pl.when(x != gx)
        def _():
            pl.semaphore_signal(barrier, inc=1, device_id=(x, gy), device_id_type=MESH)

    greet(barrier, 1)
    for n, (src, main, end) in enumerate(((b_ref, f0m, f0t), (d_ref, ddm, ddt))):
        for to, lanes in ((main, pl.ds(0, LANES)), (end, pl.ds(LANES, tail))):
            pltpu.make_async_copy(
                src.at[:, :, lanes], to.at[pl.ds(1, bx), pl.ds(ROWS, by), :], own_sem.at[n]).start()

    lane = lax.broadcasted_iota(jnp.int32, (CHUNK, LANES), 1)
    row = lax.broadcasted_iota(jnp.int32, (CHUNK, LANES), 0)

    def zeros(*shape):
        return jnp.zeros(shape, jnp.float32)

    def rolled(x, by_lanes):
        return pltpu.roll(x, by_lanes, axis=1)

    def widen(x):
        return jnp.concatenate([x, zeros(x.shape[0], LANES - tail)], 1)

    def cut(x):
        return jnp.where(lane[:x.shape[0]] < tail, x, 0.0)

    flat_f = (f0m.reshape(high * deep, LANES), f0t.reshape(high * deep, tail))
    flat_d = (ddm.reshape(high * deep, LANES), ddt.reshape(high * deep, tail))
    flat_1 = v1.reshape(2, high * deep, LANES)
    flat_2 = v2.reshape(2, high * deep, LANES)
    flat_3 = v3.reshape(2, bx * by, LANES)

    def along(at, k=0, size=None):
        return pl.ds((k + 1) * deep + at, size or bx, stride=deep)

    def strip_f(t, at):
        return widen(flat_f[1][along(at)]) if t else flat_f[0][along(at)]

    def strip_d(t, at, k=0, size=None):
        rows = along(at, k, size)
        return widen(flat_d[1][rows]) if t else flat_d[0][rows]

    for at in (first - 1, last + 1):
        flat_f[0][along(at)] = zeros(bx, LANES)
        flat_f[1][along(at)] = zeros(bx, tail)
        for t in two:
            flat_1[t, along(at)] = zeros(bx, LANES)
            flat_2[t, along(at)] = zeros(bx, LANES)
            ex[t, at:at + 1] = zeros(1, LANES)
    for side in two:
        @pl.when(jnp.logical_not(x_ok[side]))
        def _(side=side):
            xr[side] = zeros(*xr.shape[1:])
            fx[side] = zeros(*fx.shape[1:])

        @pl.when(jnp.logical_not(y_ok[side]))
        def _(side=side):
            yr[side] = zeros(*yr.shape[1:])
            fyr[side] = zeros(*fyr.shape[1:])
    for c, (dx, dy) in enumerate(CORNERS):
        @pl.when(jnp.logical_not(there(-dx, -dy)))
        def _(c=c):
            cr[c] = zeros(*cr.shape[1:])

    def f0(t, layer, start, size):
        rows = pl.ds(start, size)
        return widen(f0t[layer, rows]) if t else f0m[layer, rows]

    def dd(t, layer, start, size):
        rows = pl.ds(start, size)
        return widen(ddt[layer, rows]) if t else ddm[layer, rows]

    def g1(t, layer, start, size):
        return v1[t, layer, pl.ds(start, size)]

    def g2(t, layer, start, size):
        return v2[t, layer, pl.ds(start, size)]

    def beside_z(a, b):
        at = lane[:a.shape[0]]
        left_a, left_b = rolled(a, 1), rolled(b, 1)
        right_a, right_b = rolled(a, LANES - 1), rolled(b, LANES - 1)
        return (jnp.where(at == 0, left_b, left_a) + jnp.where(at == LANES - 1, right_b, right_a),
                jnp.where(at == 0, left_a, left_b) + right_b)

    def times_b(shift, here, others):
        z = beside_z(*here)
        out = []
        for t in two:
            total = z[t]
            for o in others:
                total = total + o[t]
            out.append(shift[t] * here[t] - total)
        return out[0], cut(out[1])

    def apply(field, layer, start, size, steps):
        def get(layer, start):
            return [field(t, layer, start, size) for t in two]

        others = [get(layer, start - 1), get(layer, start + 1)] + [get(layer + step, start) for step in steps]
        return times_b([dd(t, layer, start, size) for t in two], get(layer, start), others)

    def within(k):
        return (1,) if k == 0 else (-1,) if k == bx - 1 else (-1, 1)

    def pack(buffer, at, main, end):
        size = main.shape[0]
        half = size // 2
        low, up = end[:half], rolled(end[half:], tail)
        buffer[at:at + size] = main
        buffer[at + size:at + size + half] = jnp.where(
            lax.broadcasted_iota(jnp.int32, (half, LANES), 1) < tail, low, up)

    def unpack(buffer, at, size):
        half = size // 2
        both = buffer[at + size:at + size + half]
        keep = lax.broadcasted_iota(jnp.int32, (half, LANES), 1) < tail
        end = [jnp.where(keep, e, 0.0) for e in (both, rolled(both, LANES - tail))]
        return buffer[at:at + size], jnp.concatenate(end, 0)

    part_x, part_y = by * 9 // 4, bx * 9 // 4

    def x_copies(d, piece):
        rows = pl.ds(piece * part_x, part_x)
        return [pltpu.make_async_remote_copy(
            src_ref=xs.at[d, rows], dst_ref=xr.at[d, rows], send_sem=x_send.at[0], recv_sem=x_recv.at[d],
            device_id=(gx + 1 - 2 * d, gy), device_id_type=MESH)]

    def y_copies(d, piece):
        rows = pl.ds(piece * part_y, part_y)
        return [pltpu.make_async_remote_copy(
            src_ref=ys.at[d, rows], dst_ref=yr.at[d, rows], send_sem=y_send.at[0], recv_sem=y_recv.at[0],
            device_id=(gx, gy + 1 - 2 * d), device_id_type=MESH)]

    def start(make, at):
        @pl.when(at)
        def _():
            for copy in make():
                copy.start()

    def wait_all(ref, present, sizes, semaphore):
        for n in sizes:
            @pl.when(present == n)
            def _(n=n):
                some = ref.at[pl.ds(0, n)]
                pltpu.make_async_copy(some, some, semaphore.at[0]).wait()

    for n, ref in enumerate((b_ref, d_ref)):
        pltpu.make_async_copy(ref, ref, own_sem.at[n]).wait()

    for d in two:
        edge = x_side[1 - d][1]
        half = first + d * x_half
        pack(xs.at[d], 0, f0m[edge, first:first + by], widen(f0t[edge, first:first + by]))
        pack(xs.at[d], by * 3 // 2, ddm[edge, half:half + x_half], widen(ddt[edge, half:half + x_half]))
        edge = y_side[1 - d][1]
        pack(ys.at[d], 0, *(strip_f(t, edge) for t in two))
        pack(ys.at[d], bx * 3 // 2, *(strip_d(t, edge, d * y_half, y_half) for t in two))

    greeted(barrier, 1, nx - 1)
    for d in two:
        start(functools.partial(x_copies, d, 0), x_ok[1 - d])
        start(functools.partial(y_copies, d, 0), y_ok[1 - d])

    stages = relay_reaches(ny)
    entered = [0]

    def enter():
        n = entered[0]
        if 0 < n <= len(stages):
            greeted(ready.at[n - 1], stages[n - 1])
        if n < len(stages):
            greet(ready.at[n], stages[n])
        entered[0] += 1

    enter()

    for k in sorted(range(bx), key=lambda k: min(k, bx - 1 - k)):
        for at in range(first, first + by, CHUNK):
            out = apply(f0, k + 1, at, CHUNK, within(k))
            for t in two:
                v1[t, k + 1, pl.ds(at, CHUNK)] = out[t]
    for d in two:
        _, edge, inner = x_side[1 - d]
        half = first + d * x_half
        pack(xs.at[d], part_x, *(v1[t, edge, first:first + by] for t in two))
        pack(xs.at[d], part_x + by * 3 // 2, *(v1[t, inner, half:half + x_half] for t in two))
        _, edge, inner = y_side[1 - d]
        pack(ys.at[d], part_y, *(flat_1[t, along(edge)] for t in two))
        pack(ys.at[d], part_y + bx * 3 // 2, *(flat_1[t, along(inner, d * y_half, y_half)] for t in two))
    for c, (dx, dy) in enumerate(CORNERS):
        _, edge, inner = x_side[dx > 0]
        _, near, next_ = y_side[dy > 0]
        for n, (field, layer, at) in enumerate(
                ((f0, edge, near), (g1, edge, near), (f0, inner, near), (f0, edge, next_))):
            for t in two:
                cs[c, 4 * t + n:4 * t + n + 1] = field(t, layer, at, 1)
    for d in two:
        start(functools.partial(x_copies, d, 1), x_ok[1 - d])
        start(functools.partial(y_copies, d, 1), y_ok[1 - d])
    sums = [zeros(8, LANES)] * 6

    def add(n, a, b):
        total = sums[n]
        for t in two:
            product = a[t] * b[t]
            for g in range(product.shape[0] // 8):
                total = total + product[8 * g:8 * g + 8]
        sums[n] = total

    def moments(k, which, begin, end, size=CHUNK):
        layer = k + 1
        for at in range(first + begin, first + end, size):
            fields = {}

            def get(n):
                if n not in fields:
                    fields[n] = [(f0, g1, g2)[n](t, layer, at, size) for t in two]
                return fields[n]

            for n in which:
                if n < 5:
                    add(n, get(n // 2), get((n + 1) // 2))
                else:
                    a, b = get(2)
                    left_a, left_b = rolled(a, 1), rolled(b, 1)
                    edge = lane[:size] == 0
                    z = (jnp.where(edge, left_b, left_a), jnp.where(edge, left_a, left_b))
                    value = []
                    for t in two:
                        other = z[t] + g2(t, layer, at - 1, size)
                        if k > 2:
                            other = other + g2(t, layer - 1, at, size)
                        value.append(dd(t, layer, at, size) * get(2)[t] - (other + other))
                    add(5, get(2), value)

    for k in range(bx):
        for at in range(first, first + by, CHUNK):
            out = apply(g1, k + 1, at, CHUNK, within(k))
            for t in two:
                v2[t, k + 1, pl.ds(at, CHUNK)] = out[t]
        moments(k, (0,), 0, by)
    enter()
    for c, (dx, dy) in enumerate(CORNERS):
        start(lambda: [pltpu.make_async_remote_copy(
            src_ref=cs.at[c], dst_ref=cr.at[c], send_sem=c_send.at[0], recv_sem=c_recv.at[int(dx < 0)],
            device_id=(gx + dx, gy + dy), device_id_type=MESH)], there(dx, dy))

    def which(k):
        return (1, 2) + ((3, 4, 5) if 1 < k < bx - 2 else ())

    for k in range(1, bx - 1):
        moments(k, which(k), 8, by - 8)

    def corner(c, n):
        return [cr[c, 4 * t + n:4 * t + n + 1] for t in two]

    wait_all(yr, y_count, (1, 2), y_recv)
    for side in two:
        _, edge, inner = y_side[side]
        e, g = unpack(yr.at[side], 0, bx), unpack(yr.at[side], part_y, bx)
        field = [strip_f(t, edge) for t in two]
        f1h = [jnp.where(y_ok[side], g[t] - field[t], 0.0) for t in two]
        shift = lambda x: [jnp.concatenate([zeros(1, LANES), x[:-1]], 0), jnp.concatenate([x[1:], zeros(1, LANES)], 0)]
        moved = [shift(x) for x in e]
        spread = times_b([strip_d(t, edge) for t in two], e, [[m[n] for m in moved] for n in two])
        for t in two:
            flat_1[t, along(edge)] = flat_1[t, along(edge)] - e[t]
            flat_2[t, along(edge)] = flat_2[t, along(edge)] - spread[t] - f1h[t]
            flat_2[t, along(inner)] = flat_2[t, along(inner)] + e[t]
            ey[side, t] = e[t]
            hy[side, t, 1:bx + 1] = f1h[t]
    for begin in (0, by - 8):
        for k in range(1, bx - 1):
            moments(k, which(k), begin, begin + 8, 8)

    def x_phase(turn, carry):
        sums[:] = carry
        odd = lax.rem(gx, 2)
        side = jnp.where(turn == 0, 1 - odd, odd)
        upper = side == 1

        def either(low, up):
            return jnp.where(upper, up, low)

        ok = either(gx, nx - 1 - gx) > 0
        halo, edge, inner, third = (either(n, bx + 1 - n) for n in range(4))
        beyond, near = either(first - 1, last + 1), either(first, last)
        ok_y = either(gy, ny - 1 - gy) > 0

        @pl.when(ok)
        def _():
            pltpu.make_async_copy(xr.at[0], xr.at[0], x_recv.at[side]).wait()
            for n in (1, 2):
                @pl.when(y_count == n)
                def _(n=n):
                    some = cr.at[pl.ds(0, n)]
                    pltpu.make_async_copy(some, some, c_recv.at[side]).wait()

        e, g = unpack(xr.at[side], 0, by), unpack(xr.at[side], part_x, by)
        for t in two:
            ex[t, pl.ds(first, by)] = e[t]
        for at in range(0, by, CHUNK):
            rows = pl.ds(first + at, CHUNK)
            here = [x[at:at + CHUNK] for x in e]
            others = [[ex[t, pl.ds(first + at + step, CHUNK)] for t in two] for step in (-1, 1)]
            spread = times_b([dd(t, edge, first + at, CHUNK) for t in two], here, others)
            for t in two:
                f1h = jnp.where(ok, g[t][at:at + CHUNK] - f0(t, edge, first + at, CHUNK), 0.0)
                v1[t, halo, rows] = f1h
                v1[t, edge, rows] = v1[t, edge, rows] - here[t]
                v2[t, edge, rows] = v2[t, edge, rows] - spread[t] - f1h
                v2[t, inner, rows] = v2[t, inner, rows] + here[t]
        for c, at in ((side, near), (side + 2, first + last - near)):
            for t in two:
                p = corner(c, 0)[t]
                v1[t, halo, pl.ds(at, 1)] = v1[t, halo, pl.ds(at, 1)] - p
                v2[t, edge, pl.ds(at, 1)] = v2[t, edge, pl.ds(at, 1)] + (p + p)
        for t in two:
            value = corner(side, 1)[t] - ey[side, t, pl.ds(edge - 1, 1)] - ex[t, pl.ds(near, 1)]
            value = jnp.where(ok & ok_y, value, 0.0)
            v1[t, halo, pl.ds(beyond, 1)] = value
            hy[side, t, pl.ds(halo, 1)] = value
            hy[side, t, pl.ds(edge, 1)] = hy[side, t, pl.ds(edge, 1)] - corner(side, 0)[t]
        shift = unpack(xr.at[side], by * 3 // 2, x_half)
        far = unpack(xr.at[side], part_x + by * 3 // 2, x_half)
        more = corner(side, 2)
        for at in range(0, x_half, CHUNK):
            begin = first + side * x_half + at
            others = [[g1(t, halo, begin + step, CHUNK) for t in two] for step in (-1, 1)]
            others += [[g1(t, edge, begin, CHUNK) for t in two], [x[at:at + CHUNK] for x in far]]
            out = times_b([x[at:at + CHUNK] for x in shift], [g1(t, halo, begin, CHUNK) for t in two], others)
            value = []
            for t in two:
                o = out[t] + jnp.where(row + begin == near, more[t], 0.0)
                o = jnp.where(ok, o, 0.0)
                fx[side, t, pl.ds(begin - first, CHUNK)] = o
                value.append(o)
            add(5, [-2.0 * g2(t, edge, begin, CHUNK) for t in two], value)
        k = side * y_half
        shift = unpack(yr.at[side], bx * 3 // 2, y_half)
        far = unpack(yr.at[side], part_y + bx * 3 // 2, y_half)
        here, *moved = [[hy[side, t, pl.ds(k + step, y_half)] for t in two] for step in (1, 0, 2)]
        inside = [flat_1[t, along(near, k, y_half)] for t in two]
        out = times_b(shift, here, moved + [inside, far])
        value = []
        for t in two:
            o = out[t] + jnp.where(row[:y_half] + k == edge - 1, corner(side, 3)[t], 0.0)
            o = jnp.where(ok_y, o, 0.0)
            fy[side, t] = o
            value.append(o)
        add(5, [-2.0 * flat_2[t, along(near, k, y_half)] for t in two], value)

        for at in range(first, first + by, CHUNK):
            zero, one, two_e, two_i = (
                [field(t, layer, at, CHUNK) for t in two]
                for field, layer in ((f0, edge), (g1, edge), (g2, edge), (g2, inner)))
            one_i, two_t = ([field(t, layer, at, CHUNK) for t in two] for field, layer in ((g1, inner), (g2, third)))
            add(1, zero, one)
            add(2, one, one)
            for layer, f1_, f2_, next_ in ((edge, one, two_e, two_i), (inner, one_i, two_i, two_t)):
                add(3, f1_, f2_)
                add(4, f2_, f2_)
                left_a, left_b = rolled(f2_[0], 1), rolled(f2_[1], 1)
                z = (jnp.where(lane == 0, left_b, left_a), jnp.where(lane == 0, left_a, left_b))
                value = []
                for t in two:
                    other = z[t] + g2(t, layer, at - 1, CHUNK) + next_[t]
                    value.append(dd(t, layer, at, CHUNK) * f2_[t] - (other + other))
                add(5, f2_, value)
        return tuple(sums)

    sums[:] = lax.fori_loop(0, 2, x_phase, tuple(sums))

    while entered[0] <= len(stages):
        enter()
    lane_of = lane[:8]
    row_of = row[:8]
    stacked = zeros(8, LANES)
    for n, s in enumerate(sums):
        stacked = jnp.where(row_of == n, jnp.sum(s, 0, keepdims=True), stacked)
    packed = jnp.sum(jnp.where(lane_of == row_of, jnp.sum(stacked, 1, keepdims=True), 0.0), 0, keepdims=True)
    part[...] = packed

    @pl.loop(0, nx, unroll=nx * ny <= 64)
    def _(x):
        @pl.loop(0, ny, unroll=nx * ny <= 64)
        def _(y):
            @pl.when((x != gx) | (y != gy))
            def _():
                pltpu.make_async_remote_copy(
                    src_ref=part, dst_ref=slots.at[pl.ds(me, 1)], send_sem=sum_send.at[0],
                    recv_sem=sum_recv.at[0], device_id=(x, y), device_id_type=MESH).start()

    slots[pl.ds(me, 1)] = packed
    for d in two:
        _, edge, _ = x_side[1 - d]
        rows = pl.ds((1 - d) * x_half, x_half)
        start(lambda: [pltpu.make_async_remote_copy(
            src_ref=v2.at[:, edge, pl.ds(first + (1 - d) * x_half, x_half)], dst_ref=fx.at[d, :, rows],
            send_sem=fx_send.at[0], recv_sem=fx_recv.at[0],
            device_id=(gx + 1 - 2 * d, gy), device_id_type=MESH)], x_ok[1 - d])
        _, edge, _ = y_side[1 - d]
        for t in two:
            fys[d, t] = flat_2[t, along(edge, (1 - d) * y_half, y_half)]
        start(lambda: [pltpu.make_async_remote_copy(
            src_ref=fys.at[d], dst_ref=fyr.at[d], send_sem=fy_send.at[0], recv_sem=fy_recv.at[0],
            device_id=(gx, gy + 1 - 2 * d), device_id_type=MESH)], y_ok[1 - d])

    for k in range(bx):
        for at in range(first, first + by, CHUNK):
            out = apply(g2, k + 1, at, CHUNK, within(k))
            for t in two:
                v3[t, k, pl.ds(at - first, CHUNK)] = out[t]

    wait_all(xs, x_count, (1, 2), x_send)
    wait_all(ys, y_count, (1, 2), y_send)
    wait_all(cs, x_count * y_count, (1, 2, 4), c_send)
    half_x, half_y = fx.at[:, :, pl.ds(0, x_half)], fys
    wait_all(half_x, x_count, (1, 2), fx_send)
    wait_all(half_y, y_count, (1, 2), fy_send)
    others = slots.at[pl.ds(0, count - 1)]
    pltpu.make_async_copy(others, others, sum_send.at[0]).wait()
    wait_all(half_x, x_count, (1, 2), fx_recv)
    wait_all(half_y, y_count, (1, 2), fy_recv)
    for side in two:
        edge = x_side[side][1] - 1
        for t in two:
            v3[t, edge] = v3[t, edge] - fx[side, t]
        edge = y_side[side][1] - first
        for t in two:
            pieces = [fy[side, t], fyr[side, t]]
            rows = pl.ds(edge, bx, stride=by)
            flat_3[t, rows] = flat_3[t, rows] - jnp.concatenate(pieces[::-1] if side else pieces, 0)

    pltpu.make_async_copy(others, others, sum_recv.at[0]).wait()
    total = jnp.sum(slots[...], 0, keepdims=True)
    moment = [jnp.broadcast_to(total[:, k:k + 1], (1, LANES)) for k in range(6)]
    co = zeros(8, LANES)
    for k, c in enumerate(coefficients(moment)):
        co = jnp.where(row_of == k, c, co)
    co_ref[...] = co


def combine(f0m, f0t, v1, v2, v3, co_ref, x_out, r_out, x_buf, r_buf, sems):
    bx, by, bz = x_out.shape
    tail = bz - LANES
    c = [jnp.broadcast_to(co_ref[k:k + 1, :], (by, LANES)) for k in range(7)]
    rows = pl.ds(ROWS, by)

    def copy(n, k):
        src, dst = ((x_buf, x_out), (r_buf, r_out))[n]
        return pltpu.make_async_copy(src.at[pl.ds(k, 1)], dst.at[pl.ds(k, 1)], sems.at[n, k])

    for k in range(bx):
        for t in range(2):
            wide = LANES if t == 0 else tail
            lanes = slice(LANES * t, LANES * t + wide)
            f0 = f0t[k + 1, rows] if t else f0m[k + 1, rows]
            f1, f2, f3 = (v1[t, k + 1, rows], v2[t, k + 1, rows], v3[t, k])
            m = [a[:, :wide] for a in c]
            f1, f2, f3 = f1[:, :wide], f2[:, :wide], f3[:, :wide]
            x_buf[k, :, lanes] = m[0] * f0 + m[1] * f1 + m[2] * f2
            r_buf[k, :, lanes] = m[3] * f0 + m[4] * f1 + m[5] * f2 + m[6] * f3
        for n in range(2):
            copy(n, k).start()
    for k in range(bx):
        for n in range(2):
            copy(n, k).wait()


def on_device(nx, ny, right_side, diagonal):
    bx, by, bz = right_side.shape
    tail = bz - LANES
    f32 = jnp.float32
    block = jax.ShapeDtypeStruct((bx, by, bz), f32)
    high, deep = bx + 2, by + 3 * ROWS
    vmem = pl.BlockSpec(memory_space=pltpu.VMEM)
    dma = pltpu.SemaphoreType.DMA
    shape = lambda *dims: jax.ShapeDtypeStruct(dims, f32)
    space = lambda *dims: pltpu.VMEM(dims, f32)
    x_rows, y_rows = by * 9 // 2, bx * 9 // 2
    fields = pl.pallas_call(
        functools.partial(kernel, nx, ny),
        out_shape=(shape(high, deep, LANES), shape(high, deep, tail), shape(2, high, deep, LANES),
                   shape(2, high, deep, LANES), shape(2, bx, by, LANES), shape(8, LANES)),
        in_specs=[pl.BlockSpec(memory_space=pltpu.HBM)] * 2,
        out_specs=(vmem,) * 6,
        scratch_shapes=[
            space(high, deep, LANES), space(high, deep, tail),
            space(2, x_rows, LANES), space(2, x_rows, LANES), space(2, y_rows, LANES), space(2, y_rows, LANES),
            space(4, 8, LANES), space(4, 8, LANES),
            space(2, deep, LANES), space(2, 2, bx, LANES), space(2, 2, bx + 2, LANES),
            space(2, 2, by, LANES), space(2, 2, bx // 2, LANES),
            space(2, 2, bx // 2, LANES), space(2, 2, bx // 2, LANES),
            space(1, LANES), space(nx * ny, LANES),
            dma((2,)), dma((1,)), dma((2,)), dma((1,)), dma((1,)), dma((1,)), dma((2,)), *[dma((1,))] * 6,
            pltpu.SemaphoreType.REGULAR((len(relay_reaches(ny)),)),
        ],
        compiler_params=pltpu.CompilerParams(
            collective_id=0, has_side_effects=True, vmem_limit_bytes=32 * 2**20),
    )(*(pltpu.with_memory_space_constraint(a, pltpu.HBM) for a in (right_side, diagonal)))
    return pl.pallas_call(
        combine,
        out_shape=(block, block),
        in_specs=[vmem] * 6,
        out_specs=(pl.BlockSpec(memory_space=pl.ANY),) * 2,
        scratch_shapes=[space(bx, by, bz), space(bx, by, bz), dma((2, bx))],
        compiler_params=pltpu.CompilerParams(vmem_limit_bytes=24 * 2**20),
    )(*fields)


def solution(mesh):
    placed = (P("gx", "gy", None), P("gx", "gy", None))
    return jax.shard_map(
        functools.partial(on_device, mesh.shape["gx"], mesh.shape["gy"]),
        mesh=mesh,
        in_specs=placed,
        out_specs=placed,
        check_vma=False,
    )
```

time: 18.5 us -> 17.1 us (0.924)
  Pallas kernels: 17.8 us -> 16.3 us
    pallas_call x1, Pallas kernels: 16.2 us -> 14.7 us  [on_device(): pl.pallas_call(functools.partial(kernel, nx, ny), out_shape=(shape(high,...]
where the time goes in v4:
time: 17.1 us; the launch traced here: 16.9 us
  Pallas kernels  16.3 us (95%)
  between operations  0.64 us (4%)
    pallas_call x1, Pallas kernels, on_device(): pl.pallas_call(functools.partial(kernel, nx, ny), out_shape=(shape(high,...  14.7 us
    pallas_call x1, Pallas kernels, on_device(): pl.pallas_call(combine, out_shape=(block, block), in_specs=[vmem] * 6, ou...  1.59 us

profile of v4, /device:TPU:0, one launch (start us, length us, event | category | flops | bytes accessed | tf_op | source)
XLA Modules:
  0.0 16.9 jit_solution(15913101691282396333)
XLA Ops:
  0.6 14.7 %shard_map.41 = (f32[18,88,128]{2,1,0:T(8,128)S(1)}, f32[18,88,64]{2,1,0:T(8,128)S(1)}, f32[2,18,88,128]{3,2,1,0:T(8,128)S(1)}, f32[2,18,88,128]{3,2,1,0:T(8,128...) custom-call(f32[16,64,192]{2,1,0:T(8,128)} %b_ref.1, f32[16,64,192]{2,1,0:T(8,128)} %d_ref.1), custom_call_target="tpu_custom_call" | custom-call | tf_op jit(solution)/shard_map/pallas_call | solution.py:557
  15.4 1.6 %shard_map.42 = (f32[16,64,192]{2,1,0:T(8,128)}, f32[16,64,192]{2,1,0:T(8,128)}) custom-call(f32[18,88,128]{2,1,0:T(8,128)S(1)} %get-tuple-element.8.f0m, f32[18,88,64]{2,1,0:T(8,128)S(1)} %get-tuple-element.9.f0t, f32[2,18,88,128]{3,2,1,0:T(8,128)S(1)} %get-tuple-element.10.v1, f32[2,18,88,128]{3,2,1,0:T(8,128)S(1)} %get-tuple-element.11.v2, ...), custom_call_target="tpu_custom_call" | custom-call | tf_op jit(solution)/shard_map/pallas_call | solution.py:577

commit v5 on v4

--- a/solution.py
+++ b/solution.py
@@ -14,6 +14,8 @@
 ROWS = 8
 LANES = 128
 CHUNK = 16
+PIECES = 4
+ORDER = (3, 0, 1, 2)
 
 
 def relay_reaches(ny):
@@ -35,8 +37,8 @@
 
 
 def kernel(nx, ny, b_ref, d_ref, f0m, f0t, v1, v2, v3, co_ref,
-           ddm, ddt, xs, xr, ys, yr, cs, cr, ex, ey, hy, fx, fy, fys, fyr, part, slots,
-           own_sem, x_send, x_recv, y_send, y_recv, c_send, c_recv,
+           ddm, ddt, xs, xr, ys, yr, cs, ex, ey, hy, fx, fy, fys, fyr, part, slots,
+           own_sem, x_send, x_recv, y_send, y_recv, c_send,
            fx_send, fx_recv, fy_send, fy_recv, sum_send, sum_recv, ready):
     gx, gy = lax.axis_index("gx"), lax.axis_index("gy")
     bx, by, bz = b_ref.shape
@@ -52,6 +54,7 @@
     x_side = ((0, 1, 2), (bx + 1, bx, bx - 1))
     y_side = ((first - 1, first, first + 1), (last + 1, last, last - 1))
     x_half, y_half = by // 2, bx // 2
+    part_x, part_y = by * 9 // 4, bx * 9 // 4
 
     def there(dx, dy):
         ok = None
@@ -78,10 +81,13 @@
             pl.semaphore_signal(barrier, inc=1, device_id=(x, gy), device_id_type=MESH)
 
     greet(barrier, 1)
-    for n, (src, main, end) in enumerate(((b_ref, f0m, f0t), (d_ref, ddm, ddt))):
-        for to, lanes in ((main, pl.ds(0, LANES)), (end, pl.ds(LANES, tail))):
-            pltpu.make_async_copy(
-                src.at[:, :, lanes], to.at[pl.ds(1, bx), pl.ds(ROWS, by), :], own_sem.at[n]).start()
+    piece = bx // PIECES
+    for c in ORDER:
+        for src, main, end in ((b_ref, f0m, f0t), (d_ref, ddm, ddt)):
+            for to, lanes in ((main, pl.ds(0, LANES)), (end, pl.ds(LANES, tail))):
+                pltpu.make_async_copy(
+                    src.at[pl.ds(c * piece, piece), :, lanes],
+                    to.at[pl.ds(1 + c * piece, piece), pl.ds(ROWS, by), :], own_sem.at[c]).start()
 
     lane = lax.broadcasted_iota(jnp.int32, (CHUNK, LANES), 1)
     row = lax.broadcasted_iota(jnp.int32, (CHUNK, LANES), 0)
@@ -132,9 +138,9 @@
             yr[side] = zeros(*yr.shape[1:])
             fyr[side] = zeros(*fyr.shape[1:])
     for c, (dx, dy) in enumerate(CORNERS):
-        @pl.when(jnp.logical_not(there(-dx, -dy)))
-        def _(c=c):
-            cr[c] = zeros(*cr.shape[1:])
+        @pl.when(x_ok[dx < 0] & jnp.logical_not(y_ok[dy < 0]))
+        def _(c=c, dx=dx):
+            xr[int(dx < 0), pl.ds(part_x * 2 + 8 * (c // 2), 8)] = zeros(8, LANES)
 
     def f0(t, layer, start, size):
         rows = pl.ds(start, size)
@@ -192,18 +198,14 @@
         end = [jnp.where(keep, e, 0.0) for e in (both, rolled(both, LANES - tail))]
         return buffer[at:at + size], jnp.concatenate(end, 0)
 
-    part_x, part_y = by * 9 // 4, bx * 9 // 4
-
-    def x_copies(d, piece):
-        rows = pl.ds(piece * part_x, part_x)
+    def x_copies(d):
         return [pltpu.make_async_remote_copy(
-            src_ref=xs.at[d, rows], dst_ref=xr.at[d, rows], send_sem=x_send.at[0], recv_sem=x_recv.at[d],
+            src_ref=xs.at[d], dst_ref=xr.at[d, pl.ds(0, part_x * 2)], send_sem=x_send.at[0], recv_sem=x_recv.at[d],
             device_id=(gx + 1 - 2 * d, gy), device_id_type=MESH)]
 
-    def y_copies(d, piece):
-        rows = pl.ds(piece * part_y, part_y)
+    def y_copies(d):
         return [pltpu.make_async_remote_copy(
-            src_ref=ys.at[d, rows], dst_ref=yr.at[d, rows], send_sem=y_send.at[0], recv_sem=y_recv.at[0],
+            src_ref=ys.at[d], dst_ref=yr.at[d], send_sem=y_send.at[0], recv_sem=y_recv.at[0],
             device_id=(gx, gy + 1 - 2 * d), device_id_type=MESH)]
 
     def start(make, at):
@@ -218,23 +220,6 @@
             def _(n=n):
                 some = ref.at[pl.ds(0, n)]
                 pltpu.make_async_copy(some, some, semaphore.at[0]).wait()
-
-    for n, ref in enumerate((b_ref, d_ref)):
-        pltpu.make_async_copy(ref, ref, own_sem.at[n]).wait()
-
-    for d in two:
-        edge = x_side[1 - d][1]
-        half = first + d * x_half
-        pack(xs.at[d], 0, f0m[edge, first:first + by], widen(f0t[edge, first:first + by]))
-        pack(xs.at[d], by * 3 // 2, ddm[edge, half:half + x_half], widen(ddt[edge, half:half + x_half]))
-        edge = y_side[1 - d][1]
-        pack(ys.at[d], 0, *(strip_f(t, edge) for t in two))
-        pack(ys.at[d], bx * 3 // 2, *(strip_d(t, edge, d * y_half, y_half) for t in two))
-
-    greeted(barrier, 1, nx - 1)
-    for d in two:
-        start(functools.partial(x_copies, d, 0), x_ok[1 - d])
-        start(functools.partial(y_copies, d, 0), y_ok[1 - d])
 
     stages = relay_reaches(ny)
     entered = [0]
@@ -247,31 +232,50 @@
             greet(ready.at[n], stages[n])
         entered[0] += 1
 
-    enter()
-
-    for k in sorted(range(bx), key=lambda k: min(k, bx - 1 - k)):
-        for at in range(first, first + by, CHUNK):
-            out = apply(f0, k + 1, at, CHUNK, within(k))
-            for t in two:
-                v1[t, k + 1, pl.ds(at, CHUNK)] = out[t]
+    def come(c):
+        some = b_ref.at[pl.ds(0, 2 * piece)]
+        pltpu.make_async_copy(some, some, own_sem.at[c]).wait()
+
+    here, done = set(), set()
+    for n, c in enumerate(ORDER):
+        come(c)
+        here |= set(range(c * piece, (c + 1) * piece))
+        for k in range(bx):
+            if k in done or not {max(k - 1, 0), k, min(k + 1, bx - 1)} <= here:
+                continue
+            done.add(k)
+            for at in range(first, first + by, CHUNK):
+                out = apply(f0, k + 1, at, CHUNK, within(k))
+                for t in two:
+                    v1[t, k + 1, pl.ds(at, CHUNK)] = out[t]
+        if n != 1:
+            continue
+        for d in two:
+            _, edge, inner = x_side[1 - d]
+            half = first + d * x_half
+            pack(xs.at[d], 0, f0m[edge, first:first + by], widen(f0t[edge, first:first + by]))
+            pack(xs.at[d], by * 3 // 2, ddm[edge, half:half + x_half], widen(ddt[edge, half:half + x_half]))
+            pack(xs.at[d], part_x, *(v1[t, edge, first:first + by] for t in two))
+            pack(xs.at[d], part_x + by * 3 // 2, *(v1[t, inner, half:half + x_half] for t in two))
+        for c, (dx, dy) in enumerate(CORNERS):
+            _, edge, inner = x_side[dx > 0]
+            _, near, next_ = y_side[dy > 0]
+            for n, (field, layer, at) in enumerate(
+                    ((f0, edge, near), (g1, edge, near), (f0, inner, near), (f0, edge, next_))):
+                for t in two:
+                    cs[c, 4 * t + n:4 * t + n + 1] = field(t, layer, at, 1)
+        greeted(barrier, 1, nx - 1)
+        for d in two:
+            start(functools.partial(x_copies, d), x_ok[1 - d])
+        enter()
     for d in two:
-        _, edge, inner = x_side[1 - d]
-        half = first + d * x_half
-        pack(xs.at[d], part_x, *(v1[t, edge, first:first + by] for t in two))
-        pack(xs.at[d], part_x + by * 3 // 2, *(v1[t, inner, half:half + x_half] for t in two))
         _, edge, inner = y_side[1 - d]
+        pack(ys.at[d], 0, *(strip_f(t, edge) for t in two))
+        pack(ys.at[d], bx * 3 // 2, *(strip_d(t, edge, d * y_half, y_half) for t in two))
         pack(ys.at[d], part_y, *(flat_1[t, along(edge)] for t in two))
         pack(ys.at[d], part_y + bx * 3 // 2, *(flat_1[t, along(inner, d * y_half, y_half)] for t in two))
-    for c, (dx, dy) in enumerate(CORNERS):
-        _, edge, inner = x_side[dx > 0]
-        _, near, next_ = y_side[dy > 0]
-        for n, (field, layer, at) in enumerate(
-                ((f0, edge, near), (g1, edge, near), (f0, inner, near), (f0, edge, next_))):
-            for t in two:
-                cs[c, 4 * t + n:4 * t + n + 1] = field(t, layer, at, 1)
-    for d in two:
-        start(functools.partial(x_copies, d, 1), x_ok[1 - d])
-        start(functools.partial(y_copies, d, 1), y_ok[1 - d])
+        start(functools.partial(y_copies, d), y_ok[1 - d])
+
     sums = [zeros(8, LANES)] * 6
 
     def add(n, a, b):
@@ -308,26 +312,26 @@
                         value.append(dd(t, layer, at, size) * get(2)[t] - (other + other))
                     add(5, get(2), value)
 
+    enter()
+    for c, (dx, dy) in enumerate(CORNERS):
+        start(lambda: [pltpu.make_async_remote_copy(
+            src_ref=cs.at[c], dst_ref=xr.at[int(dx < 0), pl.ds(part_x * 2 + 8 * (c // 2), 8)],
+            send_sem=c_send.at[0], recv_sem=x_recv.at[int(dx < 0)],
+            device_id=(gx + dx, gy + dy), device_id_type=MESH)], there(dx, dy))
     for k in range(bx):
         for at in range(first, first + by, CHUNK):
             out = apply(g1, k + 1, at, CHUNK, within(k))
             for t in two:
                 v2[t, k + 1, pl.ds(at, CHUNK)] = out[t]
         moments(k, (0,), 0, by)
-    enter()
-    for c, (dx, dy) in enumerate(CORNERS):
-        start(lambda: [pltpu.make_async_remote_copy(
-            src_ref=cs.at[c], dst_ref=cr.at[c], send_sem=c_send.at[0], recv_sem=c_recv.at[int(dx < 0)],
-            device_id=(gx + dx, gy + dy), device_id_type=MESH)], there(dx, dy))
-
     def which(k):
         return (1, 2) + ((3, 4, 5) if 1 < k < bx - 2 else ())
 
     for k in range(1, bx - 1):
         moments(k, which(k), 8, by - 8)
 
-    def corner(c, n):
-        return [cr[c, 4 * t + n:4 * t + n + 1] for t in two]
+    def corner(side, other, n):
+        return [xr[side, pl.ds(part_x * 2 + 8 * other + 4 * t + n, 1)] for t in two]
 
     wait_all(yr, y_count, (1, 2), y_recv)
     for side in two:
@@ -364,12 +368,11 @@
 
         @pl.when(ok)
         def _():
-            pltpu.make_async_copy(xr.at[0], xr.at[0], x_recv.at[side]).wait()
-            for n in (1, 2):
+            for n in (0, 1, 2):
                 @pl.when(y_count == n)
                 def _(n=n):
-                    some = cr.at[pl.ds(0, n)]
-                    pltpu.make_async_copy(some, some, c_recv.at[side]).wait()
+                    some = xr.at[0, pl.ds(0, part_x * 2 + 8 * n)]
+                    pltpu.make_async_copy(some, some, x_recv.at[side]).wait()
 
         e, g = unpack(xr.at[side], 0, by), unpack(xr.at[side], part_x, by)
         for t in two:
@@ -385,20 +388,20 @@
                 v1[t, edge, rows] = v1[t, edge, rows] - here[t]
                 v2[t, edge, rows] = v2[t, edge, rows] - spread[t] - f1h
                 v2[t, inner, rows] = v2[t, inner, rows] + here[t]
-        for c, at in ((side, near), (side + 2, first + last - near)):
+        for other, at in ((0, near), (1, first + last - near)):
             for t in two:
-                p = corner(c, 0)[t]
+                p = corner(side, other, 0)[t]
                 v1[t, halo, pl.ds(at, 1)] = v1[t, halo, pl.ds(at, 1)] - p
                 v2[t, edge, pl.ds(at, 1)] = v2[t, edge, pl.ds(at, 1)] + (p + p)
         for t in two:
-            value = corner(side, 1)[t] - ey[side, t, pl.ds(edge - 1, 1)] - ex[t, pl.ds(near, 1)]
+            value = corner(side, 0, 1)[t] - ey[side, t, pl.ds(edge - 1, 1)] - ex[t, pl.ds(near, 1)]
             value = jnp.where(ok & ok_y, value, 0.0)
             v1[t, halo, pl.ds(beyond, 1)] = value
             hy[side, t, pl.ds(halo, 1)] = value
-            hy[side, t, pl.ds(edge, 1)] = hy[side, t, pl.ds(edge, 1)] - corner(side, 0)[t]
+            hy[side, t, pl.ds(edge, 1)] = hy[side, t, pl.ds(edge, 1)] - corner(side, 0, 0)[t]
         shift = unpack(xr.at[side], by * 3 // 2, x_half)
         far = unpack(xr.at[side], part_x + by * 3 // 2, x_half)
-        more = corner(side, 2)
+        more = corner(side, 0, 2)
         for at in range(0, x_half, CHUNK):
             begin = first + side * x_half + at
             others = [[g1(t, halo, begin + step, CHUNK) for t in two] for step in (-1, 1)]
@@ -419,7 +422,7 @@
         out = times_b(shift, here, moved + [inside, far])
         value = []
         for t in two:
-            o = out[t] + jnp.where(row[:y_half] + k == edge - 1, corner(side, 3)[t], 0.0)
+            o = out[t] + jnp.where(row[:y_half] + k == edge - 1, corner(side, 0, 3)[t], 0.0)
             o = jnp.where(ok_y, o, 0.0)
             fy[side, t] = o
             value.append(o)
@@ -524,7 +527,7 @@
 
     def copy(n, k):
         src, dst = ((x_buf, x_out), (r_buf, r_out))[n]
-        return pltpu.make_async_copy(src.at[pl.ds(k, 1)], dst.at[pl.ds(k, 1)], sems.at[n, k])
+        return pltpu.make_async_copy(src.at[pl.ds(k, 1)], dst.at[pl.ds(k, 1)], sems.at[n])
 
     for k in range(bx):
         for t in range(2):
@@ -538,9 +541,8 @@
             r_buf[k, :, lanes] = m[3] * f0 + m[4] * f1 + m[5] * f2 + m[6] * f3
         for n in range(2):
             copy(n, k).start()
-    for k in range(bx):
-        for n in range(2):
-            copy(n, k).wait()
+    for n, (src, dst) in enumerate(((x_buf, x_out), (r_buf, r_out))):
+        pltpu.make_async_copy(src, dst, sems.at[n]).wait()
 
 
 def on_device(nx, ny, right_side, diagonal):
@@ -562,13 +564,13 @@
         out_specs=(vmem,) * 6,
         scratch_shapes=[
             space(high, deep, LANES), space(high, deep, tail),
-            space(2, x_rows, LANES), space(2, x_rows, LANES), space(2, y_rows, LANES), space(2, y_rows, LANES),
-            space(4, 8, LANES), space(4, 8, LANES),
+            space(2, x_rows, LANES), space(2, x_rows + 16, LANES), space(2, y_rows, LANES), space(2, y_rows, LANES),
+            space(4, 8, LANES),
             space(2, deep, LANES), space(2, 2, bx, LANES), space(2, 2, bx + 2, LANES),
             space(2, 2, by, LANES), space(2, 2, bx // 2, LANES),
             space(2, 2, bx // 2, LANES), space(2, 2, bx // 2, LANES),
             space(1, LANES), space(nx * ny, LANES),
-            dma((2,)), dma((1,)), dma((2,)), dma((1,)), dma((1,)), dma((1,)), dma((2,)), *[dma((1,))] * 6,
+            dma((PIECES,)), dma((1,)), dma((2,)), dma((1,)), dma((1,)), dma((1,)), *[dma((1,))] * 6,
             pltpu.SemaphoreType.REGULAR((len(relay_reaches(ny)),)),
         ],
         compiler_params=pltpu.CompilerParams(
@@ -579,7 +581,7 @@
         out_shape=(block, block),
         in_specs=[vmem] * 6,
         out_specs=(pl.BlockSpec(memory_space=pl.ANY),) * 2,
-        scratch_shapes=[space(bx, by, bz), space(bx, by, bz), dma((2, bx))],
+        scratch_shapes=[space(bx, by, bz), space(bx, by, bz), dma((2,))],
         compiler_params=pltpu.CompilerParams(vmem_limit_bytes=24 * 2**20),
     )(*fields)
 

time: 17.1 us -> 16.9 us (0.988)
    pallas_call x1, Pallas kernels: 1.59 us -> 1.32 us  [on_device(): pl.pallas_call(combine, out_shape=(block, block), in_specs=[vmem] * 6, ou...]
where the time goes in v5:
time: 16.9 us; the launch traced here: 16.8 us
  Pallas kernels  16.2 us (96%)
  between operations  0.64 us (4%)
    pallas_call x1, Pallas kernels, on_device(): pl.pallas_call(functools.partial(kernel, nx, ny), out_shape=(shape(high,...  14.8 us
    pallas_call x1, Pallas kernels, on_device(): pl.pallas_call(combine, out_shape=(block, block), in_specs=[vmem] * 6, ou...  1.32 us

profile of v5, /device:TPU:0, one launch (start us, length us, event | category | flops | bytes accessed | tf_op | source)
XLA Modules:
  0.0 16.8 jit_solution(2669302320367567836)
XLA Ops:
  0.6 14.8 %shard_map.41 = (f32[18,88,128]{2,1,0:T(8,128)S(1)}, f32[18,88,64]{2,1,0:T(8,128)S(1)}, f32[2,18,88,128]{3,2,1,0:T(8,128)S(1)}, f32[2,18,88,128]{3,2,1,0:T(8,128...) custom-call(f32[16,64,192]{2,1,0:T(8,128)} %b_ref.1, f32[16,64,192]{2,1,0:T(8,128)} %d_ref.1), custom_call_target="tpu_custom_call" | custom-call | tf_op jit(solution)/shard_map/pallas_call | solution.py:559
  15.5 1.3 %shard_map.42 = (f32[16,64,192]{2,1,0:T(8,128)}, f32[16,64,192]{2,1,0:T(8,128)}) custom-call(f32[18,88,128]{2,1,0:T(8,128)S(1)} %get-tuple-element.8.f0m, f32[18,88,64]{2,1,0:T(8,128)S(1)} %get-tuple-element.9.f0t, f32[2,18,88,128]{3,2,1,0:T(8,128)S(1)} %get-tuple-element.10.v1, f32[2,18,88,128]{3,2,1,0:T(8,128)S(1)} %get-tuple-element.11.v2, ...), custom_call_target="tpu_custom_call" | custom-call | tf_op jit(solution)/shard_map/pallas_call | solution.py:579

commit v6 on v5

--- a/solution.py
+++ b/solution.py
@@ -200,8 +200,9 @@
 
     def x_copies(d):
         return [pltpu.make_async_remote_copy(
-            src_ref=xs.at[d], dst_ref=xr.at[d, pl.ds(0, part_x * 2)], send_sem=x_send.at[0], recv_sem=x_recv.at[d],
-            device_id=(gx + 1 - 2 * d, gy), device_id_type=MESH)]
+            src_ref=xs.at[d, rows], dst_ref=xr.at[d, rows], send_sem=x_send.at[0], recv_sem=x_recv.at[d + 2 * n],
+            device_id=(gx + 1 - 2 * d, gy), device_id_type=MESH)
+            for n, rows in enumerate((pl.ds(0, by * 3), pl.ds(by * 3, x_half * 3)))]
 
     def y_copies(d):
         return [pltpu.make_async_remote_copy(
@@ -253,10 +254,14 @@
         for d in two:
             _, edge, inner = x_side[1 - d]
             half = first + d * x_half
-            pack(xs.at[d], 0, f0m[edge, first:first + by], widen(f0t[edge, first:first + by]))
-            pack(xs.at[d], by * 3 // 2, ddm[edge, half:half + x_half], widen(ddt[edge, half:half + x_half]))
-            pack(xs.at[d], part_x, *(v1[t, edge, first:first + by] for t in two))
-            pack(xs.at[d], part_x + by * 3 // 2, *(v1[t, inner, half:half + x_half] for t in two))
+            for at, size, one, one_at, two_, two_at in (
+                    (0, by, f0, first, edge, first), (by * 3, x_half, dd, half, inner, half)):
+                for n in range(0, size, CHUNK):
+                    a = [one(t, edge, one_at + n, CHUNK) for t in two]
+                    b = [g1(t, two_, two_at + n, CHUNK) for t in two]
+                    xs[d, pl.ds(at + n, CHUNK)] = a[0]
+                    xs[d, pl.ds(at + size + n, CHUNK)] = b[0]
+                    xs[d, pl.ds(at + 2 * size + n, CHUNK)] = jnp.where(lane < tail, a[1], rolled(b[1], tail))
         for c, (dx, dy) in enumerate(CORNERS):
             _, edge, inner = x_side[dx > 0]
             _, near, next_ = y_side[dy > 0]
@@ -371,19 +376,24 @@
             for n in (0, 1, 2):
                 @pl.when(y_count == n)
                 def _(n=n):
-                    some = xr.at[0, pl.ds(0, part_x * 2 + 8 * n)]
+                    some = xr.at[0, pl.ds(0, by * 3 + 8 * n)]
                     pltpu.make_async_copy(some, some, x_recv.at[side]).wait()
 
-        e, g = unpack(xr.at[side], 0, by), unpack(xr.at[side], part_x, by)
-        for t in two:
-            ex[t, pl.ds(first, by)] = e[t]
-        for at in range(0, by, CHUNK):
+        def got(at, size, n):
+            end = xr[side, pl.ds(at + 2 * size + n, CHUNK)]
+            return ((xr[side, pl.ds(at + n, CHUNK)], cut(end)),
+                    (xr[side, pl.ds(at + size + n, CHUNK)], cut(rolled(end, LANES - tail))))
+
+        chunks = [got(0, by, at) for at in range(0, by, CHUNK)]
+        for n, (e, _) in enumerate(chunks):
+            for t in two:
+                ex[t, pl.ds(first + n * CHUNK, CHUNK)] = e[t]
+        for at, (here, g) in zip(range(0, by, CHUNK), chunks):
             rows = pl.ds(first + at, CHUNK)
-            here = [x[at:at + CHUNK] for x in e]
             others = [[ex[t, pl.ds(first + at + step, CHUNK)] for t in two] for step in (-1, 1)]
             spread = times_b([dd(t, edge, first + at, CHUNK) for t in two], here, others)
             for t in two:
-                f1h = jnp.where(ok, g[t][at:at + CHUNK] - f0(t, edge, first + at, CHUNK), 0.0)
+                f1h = jnp.where(ok, g[t] - f0(t, edge, first + at, CHUNK), 0.0)
                 v1[t, halo, rows] = f1h
                 v1[t, edge, rows] = v1[t, edge, rows] - here[t]
                 v2[t, edge, rows] = v2[t, edge, rows] - spread[t] - f1h
@@ -399,21 +409,6 @@
             v1[t, halo, pl.ds(beyond, 1)] = value
             hy[side, t, pl.ds(halo, 1)] = value
             hy[side, t, pl.ds(edge, 1)] = hy[side, t, pl.ds(edge, 1)] - corner(side, 0, 0)[t]
-        shift = unpack(xr.at[side], by * 3 // 2, x_half)
-        far = unpack(xr.at[side], part_x + by * 3 // 2, x_half)
-        more = corner(side, 0, 2)
-        for at in range(0, x_half, CHUNK):
-            begin = first + side * x_half + at
-            others = [[g1(t, halo, begin + step, CHUNK) for t in two] for step in (-1, 1)]
-            others += [[g1(t, edge, begin, CHUNK) for t in two], [x[at:at + CHUNK] for x in far]]
-            out = times_b([x[at:at + CHUNK] for x in shift], [g1(t, halo, begin, CHUNK) for t in two], others)
-            value = []
-            for t in two:
-                o = out[t] + jnp.where(row + begin == near, more[t], 0.0)
-                o = jnp.where(ok, o, 0.0)
-                fx[side, t, pl.ds(begin - first, CHUNK)] = o
-                value.append(o)
-            add(5, [-2.0 * g2(t, edge, begin, CHUNK) for t in two], value)
         k = side * y_half
         shift = unpack(yr.at[side], bx * 3 // 2, y_half)
         far = unpack(yr.at[side], part_y + bx * 3 // 2, y_half)
@@ -445,6 +440,32 @@
                     other = z[t] + g2(t, layer, at - 1, CHUNK) + next_[t]
                     value.append(dd(t, layer, at, CHUNK) * f2_[t] - (other + other))
                 add(5, f2_, value)
+
+        parts = []
+        more = corner(side, 0, 2)
+        for at in range(0, x_half, CHUNK):
+            begin = first + side * x_half + at
+            f1h = [g1(t, halo, begin, CHUNK) for t in two]
+            z = beside_z(*f1h)
+            so_far = []
+            for t in two:
+                near_by = z[t] + g1(t, halo, begin - 1, CHUNK) + g1(t, halo, begin + 1, CHUNK)
+                near_by = near_by + g1(t, edge, begin, CHUNK)
+                so_far.append(near_by - jnp.where(row + begin == near, more[t], 0.0))
+            parts.append((begin, f1h, so_far, [-2.0 * g2(t, edge, begin, CHUNK) for t in two]))
+
+        @pl.when(ok)
+        def _():
+            some = xr.at[0, pl.ds(0, x_half * 3)]
+            pltpu.make_async_copy(some, some, x_recv.at[2 + side]).wait()
+
+        for n, (begin, f1h, so_far, weight) in enumerate(parts):
+            shift, far = got(by * 3, x_half, n * CHUNK)
+            value = [shift[t] * f1h[t] - so_far[t] - far[t] for t in two]
+            value = [jnp.where(ok, v, 0.0) for v in (value[0], cut(value[1]))]
+            for t in two:
+                fx[side, t, pl.ds(begin - first, CHUNK)] = value[t]
+            add(5, weight, value)
         return tuple(sums)
 
     sums[:] = lax.fori_loop(0, 2, x_phase, tuple(sums))
@@ -570,7 +591,7 @@
             space(2, 2, by, LANES), space(2, 2, bx // 2, LANES),
             space(2, 2, bx // 2, LANES), space(2, 2, bx // 2, LANES),
             space(1, LANES), space(nx * ny, LANES),
-            dma((PIECES,)), dma((1,)), dma((2,)), dma((1,)), dma((1,)), dma((1,)), *[dma((1,))] * 6,
+            dma((PIECES,)), dma((1,)), dma((4,)), dma((1,)), dma((1,)), dma((1,)), *[dma((1,))] * 6,
             pltpu.SemaphoreType.REGULAR((len(relay_reaches(ny)),)),
         ],
         compiler_params=pltpu.CompilerParams(

time: 16.9 us -> 16.7 us (0.988)
  Pallas kernels: 16.2 us -> 16 us
    pallas_call x1, Pallas kernels: 14.8 us -> 14.6 us  [on_device(): pl.pallas_call(functools.partial(kernel, nx, ny), out_shape=(shape(high,...]
where the time goes in v6:
time: 16.7 us; the launch traced here: 16.6 us
  Pallas kernels  16 us (96%)
  between operations  0.64 us (4%)
    pallas_call x1, Pallas kernels, on_device(): pl.pallas_call(functools.partial(kernel, nx, ny), out_shape=(shape(high,...  14.6 us
    pallas_call x1, Pallas kernels, on_device(): pl.pallas_call(combine, out_shape=(block, block), in_specs=[vmem] * 6, ou...  1.32 us

profile of v6, /device:TPU:0, one launch (start us, length us, event | category | flops | bytes accessed | tf_op | source)
XLA Modules:
  0.0 16.6 jit_solution(4293880743224987352)
XLA Ops:
  0.6 14.6 %shard_map.41 = (f32[18,88,128]{2,1,0:T(8,128)S(1)}, f32[18,88,64]{2,1,0:T(8,128)S(1)}, f32[2,18,88,128]{3,2,1,0:T(8,128)S(1)}, f32[2,18,88,128]{3,2,1,0:T(8,128...) custom-call(f32[16,64,192]{2,1,0:T(8,128)} %b_ref.1, f32[16,64,192]{2,1,0:T(8,128)} %d_ref.1), custom_call_target="tpu_custom_call" | custom-call | tf_op jit(solution)/shard_map/pallas_call | solution.py:580
  15.3 1.3 %shard_map.42 = (f32[16,64,192]{2,1,0:T(8,128)}, f32[16,64,192]{2,1,0:T(8,128)}) custom-call(f32[18,88,128]{2,1,0:T(8,128)S(1)} %get-tuple-element.8.f0m, f32[18,88,64]{2,1,0:T(8,128)S(1)} %get-tuple-element.9.f0t, f32[2,18,88,128]{3,2,1,0:T(8,128)S(1)} %get-tuple-element.10.v1, f32[2,18,88,128]{3,2,1,0:T(8,128)S(1)} %get-tuple-element.11.v2, ...), custom_call_target="tpu_custom_call" | custom-call | tf_op jit(solution)/shard_map/pallas_call | solution.py:600

commit v7 on v6

--- a/solution.py
+++ b/solution.py
@@ -197,6 +197,8 @@
         keep = lax.broadcasted_iota(jnp.int32, (half, LANES), 1) < tail
         end = [jnp.where(keep, e, 0.0) for e in (both, rolled(both, LANES - tail))]
         return buffer[at:at + size], jnp.concatenate(end, 0)
+
+    late = lax.rem(gx, 8) == 2
 
     def x_copies(d):
         return [pltpu.make_async_remote_copy(
@@ -270,8 +272,8 @@
                 for t in two:
                     cs[c, 4 * t + n:4 * t + n + 1] = field(t, layer, at, 1)
         greeted(barrier, 1, nx - 1)
-        for d in two:
-            start(functools.partial(x_copies, d), x_ok[1 - d])
+        start(functools.partial(x_copies, 0), x_ok[1])
+        start(functools.partial(x_copies, 1), x_ok[0] & jnp.logical_not(late))
         enter()
     for d in two:
         _, edge, inner = y_side[1 - d]
@@ -280,6 +282,7 @@
         pack(ys.at[d], part_y, *(flat_1[t, along(edge)] for t in two))
         pack(ys.at[d], part_y + bx * 3 // 2, *(flat_1[t, along(inner, d * y_half, y_half)] for t in two))
         start(functools.partial(y_copies, d), y_ok[1 - d])
+    start(functools.partial(x_copies, 1), late)
 
     sums = [zeros(8, LANES)] * 6
 
@@ -360,7 +363,9 @@
     def x_phase(turn, carry):
         sums[:] = carry
         odd = lax.rem(gx, 2)
-        side = jnp.where(turn == 0, 1 - odd, odd)
+        lone = (gx == 0) | (gx == nx - 1)
+        start_at = jnp.where(lone, odd, 1 - odd)
+        side = jnp.where(turn == 0, start_at, 1 - start_at)
         upper = side == 1
 
         def either(low, up):

time: 16.7 us -> 16.7 us (level)
  no operation moved by 1% of the time
where the time goes in v7:
time: 16.7 us; the launch traced here: 16.6 us
  Pallas kernels  16 us (96%)
  between operations  0.64 us (4%)
    pallas_call x1, Pallas kernels, on_device(): pl.pallas_call(functools.partial(kernel, nx, ny), out_shape=(shape(high,...  14.6 us
    pallas_call x1, Pallas kernels, on_device(): pl.pallas_call(combine, out_shape=(block, block), in_specs=[vmem] * 6, ou...  1.32 us

profile of v7, /device:TPU:0, one launch (start us, length us, event | category | flops | bytes accessed | tf_op | source)
XLA Modules:
  0.0 16.6 jit_solution(6032918242179108501)
XLA Ops:
  0.6 14.6 %shard_map.41 = (f32[18,88,128]{2,1,0:T(8,128)S(1)}, f32[18,88,64]{2,1,0:T(8,128)S(1)}, f32[2,18,88,128]{3,2,1,0:T(8,128)S(1)}, f32[2,18,88,128]{3,2,1,0:T(8,128...) custom-call(f32[16,64,192]{2,1,0:T(8,128)} %b_ref.1, f32[16,64,192]{2,1,0:T(8,128)} %d_ref.1), custom_call_target="tpu_custom_call" | custom-call | tf_op jit(solution)/shard_map/pallas_call | solution.py:585
  15.3 1.3 %shard_map.42 = (f32[16,64,192]{2,1,0:T(8,128)}, f32[16,64,192]{2,1,0:T(8,128)}) custom-call(f32[18,88,128]{2,1,0:T(8,128)S(1)} %get-tuple-element.8.f0m, f32[18,88,64]{2,1,0:T(8,128)S(1)} %get-tuple-element.9.f0t, f32[2,18,88,128]{3,2,1,0:T(8,128)S(1)} %get-tuple-element.10.v1, f32[2,18,88,128]{3,2,1,0:T(8,128)S(1)} %get-tuple-element.11.v2, ...), custom_call_target="tpu_custom_call" | custom-call | tf_op jit(solution)/shard_map/pallas_call | solution.py:605
